TPU v7x, 64 devices: a 2x2x8 block of a 4x4x8 slice. The times are simulated.
64 devices in a mesh: dp: 4 (over x, y), ep: 16 (over z, core).
Axes of the slice: x: 2, y: 2, z: 8, core: 2. Of those that a mesh axis runs over, the one named last changes fastest.
The devices are a block of a 4x4x8 slice.
Arguments:
- x_in: bfloat16 [16384, 512], P(('dp', 'ep')), parts along dimension 0
- d_out: bfloat16 [16384, 512], P(('dp', 'ep')), parts along dimension 0
- idx_a: int32 [16384, 6], P(('dp', 'ep')), parts along dimension 0
- gate_a: float32 [16384, 6], P(('dp', 'ep')), parts along dimension 0
- idx_b: int32 [16384, 6], P(('dp', 'ep')), parts along dimension 0
- gate_b: float32 [16384, 6], P(('dp', 'ep')), parts along dimension 0
- w1_a: bfloat16 [64, 512, 352], P('ep')
- w3_a: bfloat16 [64, 512, 352], P('ep')
- w2_a: bfloat16 [64, 352, 512], P('ep')
- ws1_a: bfloat16 [512, 704], replicated
- ws3_a: bfloat16 [512, 704], replicated
- ws2_a: bfloat16 [704, 512], replicated
- w1_b: bfloat16 [64, 512, 352], P('ep')
- w3_b: bfloat16 [64, 512, 352], P('ep')
- w2_b: bfloat16 [64, 352, 512], P('ep')
- ws1_b: bfloat16 [512, 704], replicated
- ws3_b: bfloat16 [512, 704], replicated
- ws2_b: bfloat16 [704, 512], replicated
Outputs:
- output 1: bfloat16 [16384, 512], P(('dp', 'ep')), parts along dimension 0
- output 2: bfloat16 [16384, 512], P(('dp', 'ep')), parts along dimension 0
- output 3: float32 [256, 512, 352], P(('dp', 'ep')), parts along dimension 0
- output 4: float32 [256, 512, 352], P(('dp', 'ep')), parts along dimension 0
- output 5: float32 [256, 352, 512], P(('dp', 'ep')), parts along dimension 0
- output 6: float32 [256, 512, 352], P(('dp', 'ep')), parts along dimension 0
- output 7: float32 [256, 512, 352], P(('dp', 'ep')), parts along dimension 0
- output 8: float32 [256, 352, 512], P(('dp', 'ep')), parts along dimension 0
- output 9: float32 [16384, 6], P(('dp', 'ep')), parts along dimension 0
- output 10: float32 [16384, 6], P(('dp', 'ep')), parts along dimension 0
There are 4 independent parts. A program takes and returns all parts, laid end to end along the dimension named above; an argument that names none is the same for every part.
All inputs are finite; a program needn't handle non-finite values.
Results may differ from a plain program's by a relative error of at most 0.0115909.
Values are sent between devices in bfloat16 or wider.
A program may use at most 768 MiB of HBM per device.

v0:
```python
import jax
import jax.numpy as jnp
from jax import lax
from jax.sharding import PartitionSpec as P


def slot_capacity(tokens, n_experts, top_k):
    return top_k * ((2 * tokens + n_experts - 1) // n_experts)


def route_tables(expert_ids, n_experts, capacity):
    flat_ids = expert_ids.reshape(-1)
    pair_count = flat_ids.shape[0]
    pair_order = jnp.argsort(flat_ids, stable=True)
    expert_count = jax.ops.segment_sum(jnp.ones_like(flat_ids), flat_ids, num_segments=n_experts)
    expert_start = jnp.cumsum(expert_count) - expert_count
    position = flat_ids * capacity + jnp.argsort(pair_order) - expert_start[flat_ids]
    slot_index = jnp.arange(capacity)
    src_pair = pair_order[jnp.minimum(expert_start[:, None] + slot_index[None, :], pair_count - 1)]
    slot_used = slot_index[None, :] < expert_count[:, None]
    return src_pair.reshape(-1), slot_used.reshape(-1), position


def to_experts(rows, group_size, capacity):
    n_local = rows.shape[0] // (group_size * capacity)
    row_shape = rows.shape[1:]
    shaped = rows.reshape((group_size, n_local, capacity) + row_shape)
    received = lax.all_to_all(shaped, 'ep', 0, 2, tiled=True)
    return received.reshape((n_local, group_size * capacity) + row_shape)


def to_sources(rows, group_size, capacity):
    n_local = rows.shape[0]
    row_shape = rows.shape[2:]
    shaped = rows.reshape((1, n_local, group_size * capacity) + row_shape)
    received = lax.all_to_all(shaped, 'ep', 2, 0, tiled=True)
    return received.reshape((group_size * n_local * capacity,) + row_shape)


def swiglu_grads(pre_gate, pre_up, d_hidden):
    sigma = jax.nn.sigmoid(pre_gate)
    d_gate = d_hidden * pre_up * sigma * (1.0 + pre_gate * (1.0 - sigma))
    d_up = d_hidden * pre_gate * sigma
    return d_gate.astype(jnp.bfloat16), d_up.astype(jnp.bfloat16)


def expert_hidden(rows, w_gate, w_up):
    pre_gate = jnp.einsum('erd,edf->erf', rows, w_gate, preferred_element_type=jnp.float32)
    pre_up = jnp.einsum('erd,edf->erf', rows, w_up, preferred_element_type=jnp.float32)
    return pre_gate, pre_up, (jax.nn.silu(pre_gate) * pre_up).astype(jnp.bfloat16)


def shared_hidden(rows, s_gate, s_up):
    pre_gate = jnp.dot(rows, s_gate, preferred_element_type=jnp.float32)
    pre_up = jnp.dot(rows, s_up, preferred_element_type=jnp.float32)
    return pre_gate, pre_up, (jax.nn.silu(pre_gate) * pre_up).astype(jnp.bfloat16)


def shared_input_grad(x_rows, d_next, s_gate, s_up, s_down):
    pre = shared_hidden(x_rows, s_gate, s_up)
    projected = jnp.einsum('td,fd->tf', d_next, s_down, preferred_element_type=jnp.float32)
    ds_gate, ds_up = swiglu_grads(pre[0], pre[1], projected)
    return (jnp.einsum('tf,df->td', ds_gate, s_gate, preferred_element_type=jnp.float32)
            + jnp.einsum('tf,df->td', ds_up, s_up, preferred_element_type=jnp.float32))


def send_rows(rows, tables, top_k, group_size, capacity):
    sent = jnp.where(tables[1][:, None], rows[tables[0] // top_k], 0)
    return to_experts(sent, group_size, capacity)


def layer_forward(x_rows, tables, gates, weights, group_size, capacity):
    w_gate, w_up, w_down, s_gate, s_up, s_down = weights
    tokens, top_k = gates.shape
    received = send_rows(x_rows, tables, top_k, group_size, capacity)
    hidden = expert_hidden(received, w_gate, w_up)[2]
    expert_out = jnp.einsum('erf,efd->erd', hidden, w_down,
                            preferred_element_type=jnp.float32).astype(jnp.bfloat16)
    returned = to_sources(expert_out, group_size, capacity)
    per_pair = returned[tables[2]].reshape(tokens, top_k, -1)
    shared = jnp.dot(shared_hidden(x_rows, s_gate, s_up)[2], s_down, preferred_element_type=jnp.float32)
    mixed = x_rows.astype(jnp.float32) + shared + jnp.sum(gates[:, :, None] * per_pair, axis=1)
    return mixed.astype(jnp.bfloat16), received


def layer_backward(x_rows, d_next, tables, gates, weights, received, group_size, capacity):
    w_gate, w_up, w_down, s_gate, s_up, s_down = weights
    tokens, top_k = gates.shape
    src_pair, slot_used, position = tables
    dy_rows = to_experts(jnp.where(slot_used[:, None], d_next[src_pair // top_k], 0), group_size, capacity)
    gate_rows = to_experts(jnp.where(slot_used, gates.reshape(-1)[src_pair], 0.0), group_size, capacity)
    pre_gate, pre_up, hidden = expert_hidden(received, w_gate, w_up)
    projected = jnp.einsum('erd,efd->erf', dy_rows, w_down, preferred_element_type=jnp.float32)
    gate_grad = jnp.sum(hidden.astype(jnp.float32) * projected, axis=2)
    scaled = (gate_rows[:, :, None] * dy_rows).astype(jnp.bfloat16)
    dw_down = jnp.einsum('erf,erd->efd', hidden, scaled, preferred_element_type=jnp.float32)
    da_gate, da_up = swiglu_grads(pre_gate, pre_up, gate_rows[:, :, None] * projected)
    dw_gate = jnp.einsum('erd,erf->edf', received, da_gate, preferred_element_type=jnp.float32)
    dw_up = jnp.einsum('erd,erf->edf', received, da_up, preferred_element_type=jnp.float32)
    d_sent = (jnp.einsum('erf,edf->erd', da_gate, w_gate, preferred_element_type=jnp.float32)
              + jnp.einsum('erf,edf->erd', da_up, w_up, preferred_element_type=jnp.float32)
              ).astype(jnp.bfloat16)
    du_back = to_sources(d_sent, group_size, capacity)
    gate_back = to_sources(gate_grad, group_size, capacity)
    du_pair = du_back[position].reshape(tokens, top_k, -1)
    d_gates = gate_back[position].reshape(tokens, top_k)
    shared_dx = shared_input_grad(x_rows, d_next, s_gate, s_up, s_down)
    d_rows = d_next.astype(jnp.float32) + shared_dx + jnp.sum(du_pair, axis=1, dtype=jnp.float32)
    return d_rows.astype(jnp.bfloat16), dw_gate, dw_up, dw_down, d_gates


def solution(mesh):
    group_size = mesh.shape['ep']
    token_spec = P(('dp', 'ep'), None)
    expert_spec = P('ep', None, None)
    shared_spec = P(None, None)
    grad_spec = P(('dp', 'ep'), None, None)
    layer_specs = (expert_spec,) * 3 + (shared_spec,) * 3

    def device_step(x_in, d_out, idx_a, gate_a, idx_b, gate_b,
                    w1_a, w3_a, w2_a, ws1_a, ws3_a, ws2_a,
                    w1_b, w3_b, w2_b, ws1_b, ws3_b, ws2_b):
        weights_a = (w1_a, w3_a, w2_a, ws1_a, ws3_a, ws2_a)
        weights_b = (w1_b, w3_b, w2_b, ws1_b, ws3_b, ws2_b)
        tokens, top_k = idx_a.shape
        n_experts = w1_a.shape[0] * group_size
        capacity = slot_capacity(tokens, n_experts, top_k)
        tables_a = route_tables(idx_a, n_experts, capacity)
        tables_b = route_tables(idx_b, n_experts, capacity)
        x_mid = layer_forward(x_in, tables_a, gate_a, weights_a, group_size, capacity)[0]
        x_last, kept_b = layer_forward(x_mid, tables_b, gate_b, weights_b, group_size, capacity)
        d_mid, dw1_b, dw3_b, dw2_b, dgate_b = layer_backward(
            x_mid, d_out, tables_b, gate_b, weights_b, kept_b, group_size, capacity)
        resent_a = send_rows(x_in, tables_a, top_k, group_size, capacity)
        d_first, dw1_a, dw3_a, dw2_a, dgate_a = layer_backward(
            x_in, d_mid, tables_a, gate_a, weights_a, resent_a, group_size, capacity)
        return (x_last, d_first, dw1_a, dw3_a, dw2_a, dw1_b, dw3_b, dw2_b, dgate_a, dgate_b)

    in_specs = (token_spec,) * 6 + layer_specs + layer_specs
    out_specs = (token_spec, token_spec) + (grad_spec,) * 6 + (token_spec, token_spec)
    return jax.shard_map(device_step, mesh=mesh, in_specs=in_specs, out_specs=out_specs, check_vma=False)
```

profile of v0, /device:TPU:21, one launch (start us, length us, event | category | flops | bytes accessed | tf_op | source)
XLA Modules:
  0.0 901.9 jit_solution(2991965398319632085)
XLA Ops:
  1.8 11.1 %scatter_custom_fusion = s32[64]{0:T(128)S(1)} fusion(s32[1536]{0:T(1024)S(1)} %reshape.854, s32[1536]{0:T(1024)S(1)} %broadcast.613, s32[]{:T(128)} %constant.46.clone.1), kind=kCustom, calls=%fused_computation.228 | custom fusion | flops 1536 | bytes 260 | tf_op jit(solution)/shard_map/scatter-add | solution.py:15
  18.5 17.4 %gather_fusion = s32[3072]{0:T(1024)S(1)} fusion(s32[1536]{0:T(1024)S(1)} %get-tuple-element.14, s32[3072]{0:T(1024)S(1)} %broadcast_clamp_fusion.5), kind=kCustom, calls=%fused_computation | custom fusion | bytes 36864 | tf_op jit(solution)/shard_map/gather | solution.py:19
  36.7 13.2 %gather_fusion.1 = bf16[3072,512]{1,0:T(8,128)(2,1)} fusion(bf16[256,512]{1,0:T(8,128)(2,1)S(1)} %copy-done.1, s32[3072]{0:T(1024)S(1)} %broadcast_clamp_fusion.1), kind=kCustom, calls=%fused_computation.1 | custom fusion | bytes 6303744 | tf_op jit(solution)/shard_map/gather | solution.py:68
  52.1 83.8 %all_to_all.185 = bf16[16,4,48,512]{3,2,1,0:T(8,128)(2,1)S(1)} all-to-all(bf16[16,4,48,512]{3,2,1,0:T(8,128)(2,1)S(1)} %broadcast_select_fusion.3), channel_id=1, replica_groups=mesh['dp'=4,'ep'=16] {'ep'}, dimensions={0} | all-to-all | bytes 6291456 | tf_op jit(solution)/shard_map/all_to_all | solution.py:28
  159.3 11.1 %scatter_custom_fusion.1 = s32[64]{0:T(128)S(1)} fusion(s32[1536]{0:T(1024)S(1)} %reshape.862, s32[1536]{0:T(1024)S(1)} %broadcast.613, s32[]{:T(128)} %constant.46.clone.1), kind=kCustom, calls=%fused_computation.226 | custom fusion | flops 1536 | bytes 260 | tf_op jit(solution)/shard_map/scatter-add | solution.py:15
  176.3 17.4 %gather_fusion.3 = s32[3072]{0:T(1024)S(1)} fusion(s32[1536]{0:T(1024)S(1)} %get-tuple-element.16, s32[3072]{0:T(1024)S(1)} %broadcast_clamp_fusion.4), kind=kCustom, calls=%fused_computation.3 | custom fusion | bytes 36864 | tf_op jit(solution)/shard_map/gather | solution.py:19
  193.9 17.4 %gather_fusion.6 = f32[3072]{0:T(1024)S(1)} fusion(f32[1536]{0:T(1024)S(1)} %reshape.580, s32[3072]{0:T(1024)S(1)} %broadcast_clamp_fusion.3), kind=kCustom, calls=%fused_computation.6 | custom fusion | bytes 36864 | tf_op jit(solution)/shard_map/gather | solution.py:91
  212.2 13.2 %gather_fusion.7 = bf16[3072,512]{1,0:T(8,128)(2,1)} fusion(bf16[256,512]{1,0:T(8,128)(2,1)S(1)} %copy-done.2, s32[3072]{0:T(1024)S(1)} %broadcast_clamp_fusion), kind=kCustom, calls=%fused_computation.7 | custom fusion | bytes 6303744 | tf_op jit(solution)/shard_map/gather | solution.py:90
  233.8 35.4 %compare_select_fusion.21 = s32[1536]{0:T(1024)S(1)} fusion(pred[1536]{0:T(1024)(128)(4,1)S(1)} %get-tuple-element.171, pred[1536]{0:T(1024)(128)(4,1)S(1)} %get-tuple-element.170, pred[1536]{0:T(1024)(128)(4,1)S(1)} %get-tuple-element.169, pred[1536]{0:T(1024)(128)(4,1)S(1)} %get-tuple-element.168, pred[1536]{0:T(1024)(128)(4,1)S(1)} %get-tuple-element.167, ...), kind=kLoop, calls=%fused_computation.211 | loop fusion | flops 96768 | bytes 112356 | tf_op jit(solution)/shard_map/select_n | solution.py:80
  284.4 7.8 gather_fusion.2
  300.4 13.2 %gather_fusion.4 = bf16[3072,512]{1,0:T(8,128)(2,1)} fusion(bf16[256,512]{1,0:T(8,128)(2,1)S(1)} %fusion.12, s32[3072]{0:T(1024)S(1)} %broadcast_clamp_fusion), kind=kCustom, calls=%fused_computation.4 | custom fusion | bytes 6303744 | tf_op jit(solution)/shard_map/gather | solution.py:68
  318.5 80.3 %all_to_all.186 = bf16[16,4,48,512]{3,2,1,0:T(8,128)(2,1)} all-to-all(bf16[16,4,48,512]{3,2,1,0:T(8,128)(2,1)} %get-tuple-element.187), channel_id=1, replica_groups=mesh['dp'=4,'ep'=16] {'ep'}, dimensions={0} | all-to-all | bytes 6291456 | tf_op jit(solution)/shard_map/all_to_all | solution.py:28
  414.8 59.0 %all-to-all-done.5 = bf16[16,4,48,512]{3,2,1,0:T(8,128)(2,1)} async-done(((bf16[16,4,48,512]{3,2,1,0:T(8,128)(2,1)}), bf16[16,4,48,512]{3,2,1,0:T(8,128)(2,1)}, u32[]{:S(2)}, u32[]{:S(2)}) %all-to-all-start.5) | async-done | bytes 3145760 | tf_op jit(solution)/shard_map/all_to_all | solution.py:28
  492.2 7.3 all-to-all-start.6
  505.0 17.4 %gather_fusion.9 = f32[3072]{0:T(1024)S(1)} fusion(f32[1536]{0:T(1024)S(1)} %reshape.584, s32[3072]{0:T(1024)S(1)} %broadcast_clamp_fusion.2), kind=kCustom, calls=%fused_computation.9 | custom fusion | bytes 36864 | tf_op jit(solution)/shard_map/gather | solution.py:91
  531.8 36.7 %compare_select_fusion.20 = s32[1536]{0:T(1024)S(1)} fusion(pred[1536]{0:T(1024)(128)(4,1)S(1)} %get-tuple-element.114, pred[1536]{0:T(1024)(128)(4,1)S(1)} %get-tuple-element.113, pred[1536]{0:T(1024)(128)(4,1)S(1)} %get-tuple-element.112, pred[1536]{0:T(1024)(128)(4,1)S(1)} %get-tuple-element.111, pred[1536]{0:T(1024)(128)(4,1)S(1)} %get-tuple-element.110, ...), kind=kLoop, calls=%fused_computation.210 | loop fusion | flops 96768 | bytes 112356 | tf_op jit(solution)/shard_map/select_n | solution.py:80
  602.9 13.2 %gather_fusion.10 = bf16[3072,512]{1,0:T(8,128)(2,1)} fusion(bf16[256,512]{1,0:T(8,128)(2,1)S(1)} %fusion.14, s32[3072]{0:T(1024)S(1)} %copy-done.54), kind=kCustom, calls=%fused_computation.10 | custom fusion | bytes 6303744 | tf_op jit(solution)/shard_map/gather | solution.py:90
  643.5 63.5 %all-to-all-done.8 = bf16[16,4,48,512]{3,2,1,0:T(8,128)(2,1)} async-done(((bf16[16,4,48,512]{3,2,1,0:T(8,128)(2,1)}), bf16[16,4,48,512]{3,2,1,0:T(8,128)(2,1)}, u32[]{:S(2)}, u32[]{:S(2)}) %all-to-all-start.8) | async-done | bytes 3145760 | tf_op jit(solution)/shard_map/all_to_all | solution.py:28
  734.7 49.8 %all-to-all-done.3 = bf16[1,4,768,512]{3,1,0,2:T(4,128)(2,1)} async-done(((bf16[1,4,768,512]{3,1,0,2:T(4,128)(2,1)}), bf16[1,4,768,512]{3,1,0,2:T(4,128)(2,1)}, u32[]{:S(2)}, u32[]{:S(2)}) %all-to-all-start.3) | async-done | bytes 3145760 | tf_op jit(solution)/shard_map/all_to_all | solution.py:36
  801.0 7.8 all-to-all-start.9
  822.2 8.4 gather_fusion.13
  835.8 7.8 gather_fusion.5
  866.7 8.6 gather_fusion.12
  883.7 7.8 gather_fusion.11
  (297 shorter events, 291.2 us)
Async XLA Ops:
  0.6 475.4 %copy-start = (bf16[4,352,512]{2,1,0:T(8,128)(2,1)S(1)}, bf16[4,352,512]{2,1,0:T(8,128)(2,1)}, u32[]{:S(2)}) copy-start(bf16[4,352,512]{2,1,0:T(8,128)(2,1)} %param.32) | copy-start | bytes 4325380
  13.0 23.6 %copy-start.59 = (s32[16,4]{1,0:T(8,128)}, s32[16,4]{1,0:T(8,128)S(1)}, u32[]{:S(2)}) copy-start(s32[16,4]{1,0:T(8,128)S(1)} %lt.140) | copy-start | bytes 772
  18.5 18.2 %copy-start.1 = (bf16[256,512]{1,0:T(8,128)(2,1)S(1)}, bf16[256,512]{1,0:T(8,128)(2,1)}, u32[]{:S(2)}) copy-start(bf16[256,512]{1,0:T(8,128)(2,1)} %param.18) | copy-start | bytes 786436
  36.6 13.3 %copy-start.53 = (s32[3072]{0:T(1024)}, s32[3072]{0:T(1024)S(1)}, u32[]{:S(2)}) copy-start(s32[3072]{0:T(1024)S(1)} %broadcast_clamp_fusion.1) | copy-start | bytes 36868
  148.7 27.4 %copy-start.67 = (f32[256,6]{0,1:T(8,128)S(1)}, f32[256,6]{0,1:T(8,128)}, u32[]{:S(2)}) copy-start(f32[256,6]{0,1:T(8,128)} %param.23) | copy-start | bytes 18436
  148.7 124.3 %all-to-all-start.1 = ((bf16[1,4,768,512]{3,1,0,2:T(4,128)(2,1)}), bf16[1,4,768,512]{3,1,0,2:T(4,128)(2,1)}, u32[]{:S(2)}, u32[]{:S(2)}) async-start(bf16[1,4,768,512]{3,1,0,2:T(4,128)(2,1)} %copy.124), calls=%async_computation.1 | async-start | bytes 6291456 | tf_op jit(solution)/shard_map/all_to_all | solution.py:36
  159.3 16.8 %copy-start.57 = (s32[1536]{0:T(1024)}, s32[1536]{0:T(1024)S(1)}, u32[]{:S(2)}) copy-start(s32[1536]{0:T(1024)S(1)} %reshape.862) | copy-start | bytes 18436
  176.2 17.6 %copy-start.29 = (f32[256,6]{1,0:T(8,128)}, f32[256,6]{1,0:T(8,128)S(1)}, u32[]{:S(2)}) copy-start(f32[256,6]{1,0:T(8,128)S(1)} %copy.127) | copy-start | bytes 18436
  193.9 18.3 %copy-start.2 = (bf16[256,512]{1,0:T(8,128)(2,1)S(1)}, bf16[256,512]{1,0:T(8,128)(2,1)}, u32[]{:S(2)}) copy-start(bf16[256,512]{1,0:T(8,128)(2,1)} %param.19) | copy-start | bytes 786436
  212.2 57.1 %copy-start.38 = (bf16[512,704]{0,1:T(8,128)(2,1)S(1)}, bf16[512,704]{0,1:T(8,128)(2,1)}, u32[]{:S(2)}) copy-start(bf16[512,704]{0,1:T(8,128)(2,1)} %param.27) | copy-start | bytes 2162692
  269.2 15.2 %copy-start.51 = (s32[2048]{0:T(1024)}, s32[2048]{0:T(1024)S(1)}, u32[]{:S(2)}) copy-start(s32[2048]{0:T(1024)S(1)} %pad_clamp_fusion.1) | copy-start | bytes 24580
  273.0 45.5 %all-to-all-start.4 = ((f32[16,1,192]{2,1,0:T(1,128)}), f32[16,1,192]{2,1,0:T(1,128)S(1)}, u32[]{:S(2)}, u32[]{:S(2)}) async-start(f32[16,1,192]{2,1,0:T(1,128)} %reshape.1284), calls=%async_computation.4 | async-start | bytes 32768 | tf_op jit(solution)/shard_map/all_to_all | solution.py:28
  398.8 75.0 %all-to-all-start.5 = ((bf16[16,4,48,512]{3,2,1,0:T(8,128)(2,1)}), bf16[16,4,48,512]{3,2,1,0:T(8,128)(2,1)}, u32[]{:S(2)}, u32[]{:S(2)}) async-start(bf16[16,4,48,512]{3,2,1,0:T(8,128)(2,1)} %get-tuple-element.188), calls=%async_computation.5 | async-start | bytes 6291456 | tf_op jit(solution)/shard_map/all_to_all | solution.py:28
  492.2 84.0 %all-to-all-start.6 = ((bf16[1,4,768,512]{3,1,0,2:T(4,128)(2,1)}), bf16[1,4,768,512]{3,1,0,2:T(4,128)(2,1)}, u32[]{:S(2)}, u32[]{:S(2)}) async-start(bf16[1,4,768,512]{3,1,0,2:T(4,128)(2,1)} %copy.137), calls=%async_computation.6 | async-start | bytes 6291456 | tf_op jit(solution)/shard_map/all_to_all | solution.py:36
  504.9 17.5 %copy-start.60 = (s32[16,4]{1,0:T(8,128)S(1)}, s32[16,4]{1,0:T(8,128)}, u32[]{:S(2)}) copy-start(s32[16,4]{1,0:T(8,128)} %copy-done.59) | copy-start | bytes 772
  504.9 26.8 %copy-start.58 = (s32[1536]{0:T(1024)S(1)}, s32[1536]{0:T(1024)}, u32[]{:S(2)}) copy-start(s32[1536]{0:T(1024)} %copy-done.57) | copy-start | bytes 18436
  504.9 65.0 %copy-start.33 = (bf16[512,704]{0,1:T(8,128)(2,1)S(1)}, bf16[512,704]{0,1:T(8,128)(2,1)}, u32[]{:S(2)}) copy-start(bf16[512,704]{0,1:T(8,128)(2,1)} %param.33) | copy-start | bytes 2162692
  576.3 39.8 %all-to-all-start.7 = ((f32[16,1,192]{2,1,0:T(1,128)}), f32[16,1,192]{2,1,0:T(1,128)}, u32[]{:S(2)}, u32[]{:S(2)}) async-start(f32[16,1,192]{2,1,0:T(1,128)} %reshape.1286), calls=%async_computation.7 | async-start | bytes 32768 | tf_op jit(solution)/shard_map/all_to_all | solution.py:28
  602.9 20.5 %copy-start.56 = (pred[16,4,48]{2,1,0:T(4,128)(4,1)S(1)}, pred[16,4,48]{2,1,0:T(4,128)(4,1)}, u32[]{:S(2)}) copy-start(pred[16,4,48]{2,1,0:T(4,128)(4,1)} %copy-done.55) | copy-start | bytes 9220
  616.1 14.4 %all-to-all-start.11 = ((f32[16,1,192]{2,1,0:T(1,128)}), f32[16,1,192]{2,1,0:T(1,128)S(1)}, u32[]{:S(2)}, u32[]{:S(2)}) async-start(f32[16,1,192]{2,1,0:T(1,128)} %reshape.1290), calls=%async_computation.11 | async-start | bytes 32768 | tf_op jit(solution)/shard_map/all_to_all | solution.py:36
  630.5 76.5 %all-to-all-start.8 = ((bf16[16,4,48,512]{3,2,1,0:T(8,128)(2,1)}), bf16[16,4,48,512]{3,2,1,0:T(8,128)(2,1)}, u32[]{:S(2)}, u32[]{:S(2)}) async-start(bf16[16,4,48,512]{3,2,1,0:T(8,128)(2,1)} %broadcast_select_fusion.2), calls=%async_computation.8 | async-start | bytes 6291456 | tf_op jit(solution)/shard_map/all_to_all | solution.py:28
  707.0 77.4 %all-to-all-start.3 = ((bf16[1,4,768,512]{3,1,0,2:T(4,128)(2,1)}), bf16[1,4,768,512]{3,1,0,2:T(4,128)(2,1)}, u32[]{:S(2)}, u32[]{:S(2)}) async-start(bf16[1,4,768,512]{3,1,0,2:T(4,128)(2,1)} %copy.131), calls=%async_computation.3 | async-start | bytes 6291456 | tf_op jit(solution)/shard_map/all_to_all | solution.py:36
  784.4 16.6 %all-to-all-start.10 = ((f32[16,1,192]{2,1,0:T(1,128)}), f32[16,1,192]{2,1,0:T(1,128)S(1)}, u32[]{:S(2)}, u32[]{:S(2)}) async-start(f32[16,1,192]{2,1,0:T(1,128)} %reshape.1288), calls=%async_computation.10 | async-start | bytes 32768 | tf_op jit(solution)/shard_map/all_to_all | solution.py:36
  801.0 78.2 %all-to-all-start.9 = ((bf16[1,4,768,512]{3,1,0,2:T(4,128)(2,1)}), bf16[1,4,768,512]{3,1,0,2:T(4,128)(2,1)}, u32[]{:S(2)}, u32[]{:S(2)}) async-start(bf16[1,4,768,512]{3,1,0,2:T(4,128)(2,1)} %copy.142), calls=%async_computation.9 | async-start | bytes 6291456 | tf_op jit(solution)/shard_map/all_to_all | solution.py:36
  (54 other events, 225.5 us)
where the time goes:
time: 913 us; the launch traced here: 902 us
  local copies, waits for them, and re-layouts  249 us (27%)
  waiting for transfers between devices  179 us (20%)
  blocking collectives  164 us (18%)
  other arithmetic  159 us (17%)
  matrix products  83.4 us (9%)
  starting transfers between devices  65.2 us (7%)
    all_to_all x2, blocking collectives, to_experts(): received = lax.all_to_all(shaped, 'ep', 0, 2, tiled=True)  164 us
    all_to_all x4, waiting for transfers between devices, to_experts(): received = lax.all_to_all(shaped, 'ep', 0, 2, tiled=True)  123 us
    select_n x2, other arithmetic, layer_forward(): per_pair = returned[tables[2]].reshape(tokens, top_k, -1)  72 us
    all_to_all x6, waiting for transfers between devices, to_sources(): received = lax.all_to_all(shaped, 'ep', 2, 0, tiled=True)  56.6 us
    all_to_all x6, starting transfers between devices, to_sources(): received = lax.all_to_all(shaped, 'ep', 2, 0, tiled=True)  40.6 us
    gather x4, local copies, waits for them, and re-layouts, layer_backward(): gates.reshape(-1)[src_pair]  35 us
    gather x2, local copies, waits for them, and re-layouts, route_tables(): pair_order[jnp.minimum(expert_start[:, None] + slot_index[None, :], pair_...  34.8 us
    gather x2, local copies, waits for them, and re-layouts, send_rows(): sent = jnp.where(tables[1][:, None], rows[tables[0] // top_k], 0)  26.4 us
  transfers between devices with their start and end apart: 10, of which 5 were waited for; matrix products, arithmetic and copies ran while one was open for 43% of the time, Pallas kernels for 0%

commit v1 on v0

v1 whole, which is shorter than its diff:
```python
import jax
import jax.numpy as jnp
from jax import lax
from jax.sharding import PartitionSpec as P

F32 = jnp.float32
BF16 = jnp.bfloat16


def slot_capacity(tokens, n_experts, top_k):
    return top_k * ((2 * tokens + n_experts - 1) // n_experts)


def swiglu_grads(pre_gate, pre_up, d_hidden):
    sigma = jax.nn.sigmoid(pre_gate)
    d_gate = d_hidden * pre_up * sigma * (1.0 + pre_gate * (1.0 - sigma))
    d_up = d_hidden * pre_gate * sigma
    return d_gate.astype(BF16), d_up.astype(BF16)


def hidden_of(rows, w_gate, w_up):
    pre_gate = jnp.matmul(rows, w_gate, preferred_element_type=F32)
    pre_up = jnp.matmul(rows, w_up, preferred_element_type=F32)
    return pre_gate, pre_up, (jax.nn.silu(pre_gate) * pre_up).astype(BF16)


def split3(values):
    hi = values.astype(BF16)
    rest = values - hi.astype(F32)
    mid = rest.astype(BF16)
    return hi, mid, (rest - mid.astype(F32)).astype(BF16)


def routing(ids, gates, n_local, capacity):
    n_src, _, tokens = ids.shape
    first = (lax.axis_index('ep') * n_local).astype(F32)
    experts = first + jnp.arange(n_local, dtype=F32)
    hit = ids[:, None] == experts[None, :, None, None]
    used = jnp.any(hit, axis=2)
    gate = jnp.sum(jnp.where(hit, gates[:, None], 0.0), axis=2)
    before = jnp.triu(jnp.ones((tokens, tokens), BF16), 1)
    rank = jnp.einsum('set,tu->seu', used.astype(BF16), before, preferred_element_type=F32)
    slot = jnp.where(used, rank, -1.0)
    match = slot[:, :, None, :] == jnp.arange(capacity, dtype=F32)[None, None, :, None]
    return match, gate


def solution(mesh):
    group_size = mesh.shape['ep']
    token_spec = P(('dp', 'ep'), None)
    expert_spec = P('ep', None, None)
    shared_spec = P(None, None)
    grad_spec = P(('dp', 'ep'), None, None)
    layer_specs = (expert_spec,) * 3 + (shared_spec,) * 3

    def dispatch(match, gathered):
        rows = jnp.einsum('sect,std->escd', match.astype(BF16), gathered, preferred_element_type=F32)
        n_local = rows.shape[0]
        return rows.astype(BF16).reshape(n_local, -1, rows.shape[-1])

    def gather(rows):
        return lax.all_gather(rows, 'ep')

    def forward(rows, match, gate, weights):
        hidden = hidden_of(rows, weights[0], weights[1])[2]
        out = jnp.matmul(hidden, weights[2], preferred_element_type=F32).astype(BF16)
        n_src, n_local, capacity, tokens = match.shape
        out = out.reshape(n_local, n_src, capacity, -1)
        part = sum(jnp.einsum('sect,escd->std', jnp.where(match, g[:, :, None, :], 0).astype(BF16), out,
                              preferred_element_type=F32) for g in split3(gate))
        return lax.psum_scatter(part, 'ep', scatter_dimension=0, tiled=True)[0]

    def backward(rows, dy, match, gate, weights):
        w_gate, w_up, w_down = weights[:3]
        n_src, n_local, capacity, tokens = match.shape
        gate_slot = jnp.sum(jnp.where(match, gate[:, :, None, :], 0.0), axis=3)
        gate_col = gate_slot.transpose(1, 0, 2).reshape(n_local, -1, 1)
        pre_gate, pre_up, hidden = hidden_of(rows, w_gate, w_up)
        projected = jnp.einsum('erd,efd->erf', dy, w_down, preferred_element_type=F32)
        gate_grad = jnp.sum(hidden.astype(F32) * projected, axis=2)
        scaled = (gate_col * dy).astype(BF16)
        dw_down = jnp.einsum('erf,erd->efd', hidden, scaled, preferred_element_type=F32)
        da_gate, da_up = swiglu_grads(pre_gate, pre_up, gate_col * projected)
        dw_gate = jnp.einsum('erd,erf->edf', rows, da_gate, preferred_element_type=F32)
        dw_up = jnp.einsum('erd,erf->edf', rows, da_up, preferred_element_type=F32)
        du = (jnp.einsum('erf,edf->erd', da_gate, w_gate, preferred_element_type=F32)
              + jnp.einsum('erf,edf->erd', da_up, w_up, preferred_element_type=F32)).astype(BF16)
        du = du.reshape(n_local, n_src, capacity, -1)
        part = jnp.einsum('sect,escd->std', match.astype(BF16), du, preferred_element_type=F32)
        du_sum = lax.psum_scatter(part, 'ep', scatter_dimension=0, tiled=True)[0]
        grad_slot = gate_grad.reshape(n_local, n_src, capacity).transpose(1, 0, 2)
        grad_tok = jnp.sum(jnp.where(match, grad_slot[:, :, :, None], 0.0), axis=2)
        grad_back = lax.all_to_all(grad_tok, 'ep', 0, 0, tiled=True)
        return du_sum, dw_gate, dw_up, dw_down, grad_back.reshape(-1, tokens)

    def gate_grads(grad_back, ids):
        experts = jnp.arange(grad_back.shape[0], dtype=ids.dtype)
        hit = ids[:, :, None] == experts[None, None, :]
        return jnp.sum(jnp.where(hit, grad_back.T[:, None, :], 0.0), axis=2)

    def shared_out(x_rows, weights):
        return jnp.matmul(hidden_of(x_rows, weights[3], weights[4])[2], weights[5], preferred_element_type=F32)

    def shared_grad(x_rows, dy, weights):
        pre_gate, pre_up, _ = hidden_of(x_rows, weights[3], weights[4])
        projected = jnp.einsum('td,fd->tf', dy, weights[5], preferred_element_type=F32)
        da_gate, da_up = swiglu_grads(pre_gate, pre_up, projected)
        return (jnp.einsum('tf,df->td', da_gate, weights[3], preferred_element_type=F32)
                + jnp.einsum('tf,df->td', da_up, weights[4], preferred_element_type=F32))

    def device_step(x_in, d_out, idx_a, gate_a, idx_b, gate_b,
                    w1_a, w3_a, w2_a, ws1_a, ws3_a, ws2_a,
                    w1_b, w3_b, w2_b, ws1_b, ws3_b, ws2_b):
        weights_a = (w1_a, w3_a, w2_a, ws1_a, ws3_a, ws2_a)
        weights_b = (w1_b, w3_b, w2_b, ws1_b, ws3_b, ws2_b)
        tokens, top_k = idx_a.shape
        n_local = w1_a.shape[0]
        capacity = slot_capacity(tokens, n_local * group_size, top_k)
        table = jnp.concatenate([idx_a.astype(F32), idx_b.astype(F32), gate_a, gate_b], axis=1).T
        tables = gather(table)
        match_a, gates_a = routing(tables[:, :top_k], tables[:, 2 * top_k:3 * top_k], n_local, capacity)
        match_b, gates_b = routing(tables[:, top_k:2 * top_k], tables[:, 3 * top_k:], n_local, capacity)
        rows_a = dispatch(match_a, gather(x_in))
        mix = forward(rows_a, match_a, gates_a, weights_a)
        x_mid = (x_in.astype(F32) + shared_out(x_in, weights_a) + mix).astype(BF16)
        rows_b = dispatch(match_b, gather(x_mid))
        mix = forward(rows_b, match_b, gates_b, weights_b)
        x_last = (x_mid.astype(F32) + shared_out(x_mid, weights_b) + mix).astype(BF16)
        dy_b = dispatch(match_b, gather(d_out))
        du_sum, dw1_b, dw3_b, dw2_b, back_b = backward(rows_b, dy_b, match_b, gates_b, weights_b)
        d_mid = (d_out.astype(F32) + shared_grad(x_mid, d_out, weights_b) + du_sum).astype(BF16)
        again = lax.optimization_barrier((x_in, du_sum))[0]
        rows_a = dispatch(match_a, gather(again))
        dy_a = dispatch(match_a, gather(d_mid))
        du_sum, dw1_a, dw3_a, dw2_a, back_a = backward(rows_a, dy_a, match_a, gates_a, weights_a)
        d_first = (d_mid.astype(F32) + shared_grad(x_in, d_mid, weights_a) + du_sum).astype(BF16)
        return (x_last, d_first, dw1_a, dw3_a, dw2_a, dw1_b, dw3_b, dw2_b,
                gate_grads(back_a, idx_a), gate_grads(back_b, idx_b))

    in_specs = (token_spec,) * 6 + layer_specs + layer_specs
    out_specs = (token_spec, token_spec) + (grad_spec,) * 6 + (token_spec, token_spec)
    return jax.shard_map(device_step, mesh=mesh, in_specs=in_specs, out_specs=out_specs, check_vma=False)
```

time: 913 us -> 560 us (0.61)
  local copies, waits for them, and re-layouts: 249 us -> 16.8 us
  waiting for transfers between devices: 179 us -> 320 us
  blocking collectives: 164 us -> 24.2 us
  other arithmetic: 159 us -> 20.1 us
  matrix products: 83.4 us -> 139 us
  starting transfers between devices: 65.2 us -> 13.8 us
  between operations: 2.07 us -> 15 us
    all_to_all x10 -> x2, waiting for transfers between devices: 179 us -> 0.01 us  [backward(): grad_back = lax.all_to_all(grad_tok, 'ep', 0, 0, tiled=True)]
    reduce_scatter x0 -> x4, waiting for transfers between devices: none -> 178 us  [the longest x2 99.4 us: backward(): du_sum = lax.psum_scatter(part, 'ep', scatter_dimension=0, tiled=True)[0]]
    gather x24 -> x0, local copies, waits for them, and re-layouts: 176 us -> none  [the longest x4 35 us: layer_backward(): gates.reshape(-1)[src_pair]]
    all_to_all x2 -> x0, blocking collectives: 164 us -> none  [to_experts(): received = lax.all_to_all(shaped, 'ep', 0, 2, tiled=True)]
    all_gather x0 -> x5, waiting for transfers between devices: none -> 140 us  [gather(): return lax.all_gather(rows, 'ep')]
    select_n x11 -> x0, other arithmetic: 83.5 us -> none  [the longest x2 72 us: layer_forward(): per_pair = returned[tables[2]].reshape(tokens, top_k, -1)]
    dot_general x30 -> x46, matrix products: 83.4 us -> 139 us  [the longest x6 25.7 us: forward(): jnp.einsum('sect,escd->std', jnp.where(match, g[:, :, None, :], 0).astype...]
    all_to_all x10 -> x2, starting transfers between devices: 65.2 us -> 12.4 us  [backward(): grad_back = lax.all_to_all(grad_tok, 'ep', 0, 0, tiled=True)]
  transfers between devices with their start and end apart: 10 -> 11, of which waited for: 5 -> 9; matrix products, arithmetic and copies ran while one was open for 43% -> 20% of each run, Pallas kernels for 0% -> 0%
where the time goes in v1:
time: 560 us; the launch traced here: 549 us
  waiting for transfers between devices  320 us (57%)
  matrix products  139 us (25%)
  blocking collectives  24.2 us (4%)
  other arithmetic  20.1 us (4%)
  local copies, waits for them, and re-layouts  16.8 us (3%)
  between operations  15 us (3%)
  starting transfers between devices  13.8 us (2%)
    all_gather x5, waiting for transfers between devices, gather(): return lax.all_gather(rows, 'ep')  140 us
    reduce_scatter x2, waiting for transfers between devices, backward(): du_sum = lax.psum_scatter(part, 'ep', scatter_dimension=0, tiled=True)[0]  99.4 us
    reduce_scatter x2, waiting for transfers between devices, forward(): return lax.psum_scatter(part, 'ep', scatter_dimension=0, tiled=True)[0]  78.5 us
    dot_general x6, matrix products, forward(): jnp.einsum('sect,escd->std', jnp.where(match, g[:, :, None, :], 0).astype...  25.7 us
    all_gather x1, blocking collectives, gather(): return lax.all_gather(rows, 'ep')  24.2 us
    dot_general x5, matrix products, dispatch(): jnp.einsum('sect,std->escd', match.astype(BF16), gathered, preferred_elem...  16 us
    unnamed x94, local copies, waits for them, and re-layouts  13 us
    dot_general x2, matrix products, forward(): jnp.matmul(hidden, weights[2], preferred_element_type=F32).astype(BF16)  12.4 us
  transfers between devices with their start and end apart: 11, of which 9 were waited for; matrix products, arithmetic and copies ran while one was open for 20% of the time, Pallas kernels for 0%

profile of v1, /device:TPU:21, one launch (start us, length us, event | category | flops | bytes accessed | tf_op | source)
XLA Modules:
  0.0 549.0 jit_solution(13630479015459583328)
XLA Ops:
  10.2 24.2 %all-gather = f32[384,256]{1,0:T(8,128)S(1)} all-gather(f32[24,256]{1,0:T(8,128)S(1)} %maximum_bitcast_fusion), channel_id=2, replica_groups=mesh['dp'=4,'ep'=16] {'ep'}, dimensions={0}, use_global_device_ids=true | all-gather | bytes 417792 | tf_op jit(solution)/shard_map/all_gather | solution.py:62
  35.9 18.0 %all-gather.12.cloned.1.call-done = bf16[4096,512]{1,0:T(8,128)(2,1)} async-done(((bf16[256,512]{1,0:T(8,128)(2,1)}), bf16[4096,512]{1,0:T(8,128)(2,1)}) %all-gather.12.cloned.1.call-update) | async-done | bytes 4194320 | tf_op jit(solution)/shard_map/all_gather | solution.py:62
  62.3 8.5 %convolution_convert_fusion.1 = bf16[4,768,512]{2,1,0:T(8,128)(2,1)} fusion(bf16[4,352,512]{2,1,0:T(8,128)(2,1)} %param.26, f32[4,768,352]{1,2,0:T(8,128)} %fusion.106, bf16[4,768,512]{2,1,0:T(8,128)(2,1)} %bitcast.166, bf16[4,512,352]{1,2,0:T(8,128)(2,1)S(1)} %copy-done), kind=kOutput, calls=%fused_computation.60 | convolution fusion | flops 2222653440 | bytes 13500416 | tf_op jit(solution)/shard_map/dot_general | solution.py:66
  75.7 6.7 %bitcast_add_fusion.2 = f32[16,256,512]{2,1,0:T(8,128)} fusion(f32[16,256,512,1]{2,1,3,0:T(8,128)S(1)} %fusion.23, f32[16,256,512,1]{2,1,3,0:T(8,128)S(1)} %fusion.25, bf16[4,16,48,512]{3,2,1,0:T(8,128)(2,1)} %bitcast.179, f32[16,4,256]{2,1,0:T(4,128)S(1)} %copy.106, bf16[16,4,256]{2,1,0:T(4,128)(2,1)S(1)} %copy.113), kind=kOutput, calls=%fused_computation.2 | convolution fusion | flops 811073536 | bytes 28409856 | tf_op jit(solution)/shard_map/sect,escd->std/dot_general | solution.py:69
  88.1 57.3 %reduce-scatter.5.cloned.1.call-done = f32[1,256,512]{2,1,0:T(8,128)} async-done(((f32[16,256,512]{2,1,0:T(8,128)}), f32[1,256,512]{2,1,0:T(8,128)}) %reduce-scatter.5.cloned.1.call-update) | async-done | bytes 524304 | tf_op jit(solution)/shard_map/reduce_scatter | solution.py:71
  149.0 38.6 %all-gather.16.cloned.1.call-done = bf16[4096,512]{1,0:T(8,128)(2,1)} async-done(((bf16[256,512]{1,0:T(8,128)(2,1)}), bf16[4096,512]{1,0:T(8,128)(2,1)}) %all-gather.16.cloned.1.call-update) | async-done | bytes 4194320 | tf_op jit(solution)/shard_map/all_gather | solution.py:62
  192.8 33.8 %all-gather.14.cloned.1.call-done = bf16[4096,512]{1,0:T(8,128)(2,1)} async-done(((bf16[256,512]{1,0:T(8,128)(2,1)}), bf16[4096,512]{1,0:T(8,128)(2,1)}) %all-gather.14.cloned.1.call-update) | async-done | bytes 4194320 | tf_op jit(solution)/shard_map/all_gather | solution.py:62
  244.1 5.9 %multiply_convert_fusion.5 = (bf16[4,768,352]{1,2,0:T(8,128)(2,1)S(1)}, bf16[4,768,352]{1,2,0:T(8,128)(2,1)S(1)}) fusion(f32[4,768,352]{1,2,0:T(8,128)} %copy-done.12, f32[4,768,352]{1,2,0:T(8,128)} %get-tuple-element.38, f32[4,768]{1,0:T(4,128)S(1)} %mul.167, f32[4,768,352]{1,2,0:T(8,128)} %copy-done.13), kind=kLoop, calls=%fused_computation.14 | loop fusion | flops 15138816 | bytes 17313792 | tf_op jit(solution)/shard_map/convert_element_type | solution.py:18
  254.4 4.7 convolution_bitcast_fusion.1
  266.5 55.3 %reduce-scatter.9.cloned.1.call-done = f32[1,256,512]{2,1,0:T(8,128)} async-done(((f32[16,256,512]{2,1,0:T(8,128)}), f32[1,256,512]{2,1,0:T(8,128)}) %reduce-scatter.9.cloned.1.call-update) | async-done | bytes 524304 | tf_op jit(solution)/shard_map/reduce_scatter | solution.py:90
  325.1 3.9 convolution_convert_fusion
  330.4 4.6 fusion.18
  335.0 8.2 %bitcast_add_fusion = f32[16,256,512]{2,1,0:T(8,128)} fusion(f32[16,256,512,1]{2,1,3,0:T(8,128)} %fusion.18, f32[16,256,512,1]{2,1,3,0:T(8,128)S(1)} %fusion.20, bf16[4,16,48,512]{3,2,1,0:T(8,128)(2,1)S(1)} %bitcast.169, f32[16,4,256]{2,1,0:T(4,128)S(1)} %copy.116, bf16[16,4,256]{2,1,0:T(4,128)(2,1)S(1)} %copy.123), kind=kOutput, calls=%fused_computation | convolution fusion | flops 811073536 | bytes 28409856 | tf_op jit(solution)/shard_map/sect,escd->std/dot_general | solution.py:69
  343.6 20.5 %all-gather.20.cloned.1.call-done = bf16[4096,512]{1,0:T(8,128)(2,1)} async-done(((bf16[256,512]{1,0:T(8,128)(2,1)}), bf16[4096,512]{1,0:T(8,128)(2,1)}) %all-gather.20.cloned.1.call-update) | async-done | bytes 4194320 | tf_op jit(solution)/shard_map/all_gather | solution.py:62
  374.3 28.8 %all-gather.18.cloned.1.call-done = bf16[4096,512]{1,0:T(8,128)(2,1)} async-done(((bf16[256,512]{1,0:T(8,128)(2,1)}), bf16[4096,512]{1,0:T(8,128)(2,1)}) %all-gather.18.cloned.1.call-update) | async-done | bytes 4194320 | tf_op jit(solution)/shard_map/all_gather | solution.py:62
  410.3 3.7 multiply_reduce_fusion.1
  416.1 5.8 %multiply_convert_fusion.3 = (bf16[4,768,352]{1,2,0:T(8,128)(2,1)S(1)}, bf16[4,768,352]{1,2,0:T(8,128)(2,1)S(1)}) fusion(f32[4,768,352]{1,2,0:T(8,128)} %fusion.115, f32[4,768,352]{1,2,0:T(8,128)} %get-tuple-element.39, f32[4,768]{1,0:T(4,128)S(1)} %mul.182, f32[4,768,352]{1,2,0:T(8,128)} %fusion.114), kind=kLoop, calls=%fused_computation.11 | loop fusion | flops 15138816 | bytes 17313792 | tf_op jit(solution)/shard_map/convert_element_type | solution.py:18
  425.8 4.6 convolution_bitcast_fusion
  430.5 4.4 all-to-all-start.1
  434.9 5.6 %fusion.119 = f32[4,512,352]{1,2,0:T(8,128)} fusion(bf16[4,768,352]{1,2,0:T(8,128)(2,1)} %copy-done.7, bf16[4,768,512]{2,1,0:T(8,128)(2,1)} %bitcast.157), kind=kOutput, calls=%fused_computation.174 | convolution fusion | flops 1107296256 | bytes 8192000 | tf_op jit(solution)/shard_map/erd,erf->edf/dot_general | solution.py:84
  448.3 21.3 %reduce-scatter.7.cloned.1.call-done = f32[1,256,512]{2,1,0:T(8,128)} async-done(((f32[16,256,512]{2,1,0:T(8,128)}), f32[1,256,512]{2,1,0:T(8,128)}) %reduce-scatter.7.cloned.1.call-update) | async-done | bytes 524304 | tf_op jit(solution)/shard_map/reduce_scatter | solution.py:71
  475.1 8.0 %all-to-all-start = ((f32[16,4,256]{2,1,0:T(4,128)}), f32[16,4,256]{2,1,0:T(4,128)S(1)}, u32[]{:S(2)}, u32[]{:S(2)}) async-start(f32[16,4,256]{2,1,0:T(4,128)} %get-tuple-element.14), calls=%async_computation.4 | async-start | bytes 131072 | tf_op jit(solution)/shard_map/all_to_all | solution.py:93
  483.2 5.6 %fusion.117 = f32[4,512,352]{1,2,0:T(8,128)} fusion(bf16[4,768,352]{1,2,0:T(8,128)(2,1)} %copy-done.10, bf16[4,768,512]{2,1,0:T(8,128)(2,1)} %bitcast.161), kind=kOutput, calls=%fused_computation.172 | convolution fusion | flops 1107296256 | bytes 8192000 | tf_op jit(solution)/shard_map/erd,erf->edf/dot_general | solution.py:84
  495.3 44.1 %reduce-scatter.11.cloned.1.call-done = f32[1,256,512]{2,1,0:T(8,128)} async-done(((f32[16,256,512]{2,1,0:T(8,128)}), f32[1,256,512]{2,1,0:T(8,128)}) %reduce-scatter.11.cloned.1.call-update) | async-done | bytes 524304 | tf_op jit(solution)/shard_map/reduce_scatter | solution.py:90
  (192 shorter events, 111.9 us)
Async XLA Ops:
  7.2 55.1 %copy-start = (bf16[4,512,352]{1,2,0:T(8,128)(2,1)S(1)}, bf16[4,512,352]{1,2,0:T(8,128)(2,1)}, u32[]{:S(2)}) copy-start(bf16[4,512,352]{1,2,0:T(8,128)(2,1)} %param.25) | copy-start | bytes 4325380
  7.2 46.7 %all-gather.12.cloned.1.call-start = ((), (), s32[]{:S(2)}) async-start(), calls=%async_computation.10 | async-start | bytes 4456448 | tf_op jit(solution)/shard_map/all_gather | solution.py:62
  8.0 137.4 %reduce-scatter.5.cloned.1.call-start = ((), (), s32[]{:S(2)}) async-start(), calls=%async_computation.6 | async-start | bytes 8912896 | tf_op jit(solution)/shard_map/reduce_scatter | solution.py:71
  82.4 105.2 %all-gather.16.cloned.1.call-start = ((), (), s32[]{:S(2)}) async-start(), calls=%async_computation.12 | async-start | bytes 4456448 | tf_op jit(solution)/shard_map/all_gather | solution.py:62
  83.2 143.3 %all-gather.14.cloned.1.call-start = ((), (), s32[]{:S(2)}) async-start(), calls=%async_computation.11 | async-start | bytes 4456448 | tf_op jit(solution)/shard_map/all_gather | solution.py:62
  148.2 173.6 %reduce-scatter.9.cloned.1.call-start = ((), (), s32[]{:S(2)}) async-start(), calls=%async_computation.8 | async-start | bytes 8912896 | tf_op jit(solution)/shard_map/reduce_scatter | solution.py:90
  234.3 7.7 %copy-start.13 = (f32[4,768,352]{1,2,0:T(8,128)}, f32[4,768,352]{1,2,0:T(8,128)S(1)}, u32[]{:S(2)}) copy-start(f32[4,768,352]{1,2,0:T(8,128)S(1)} %fusion.110) | copy-start | bytes 12976132
  244.1 6.0 %copy-start.17 = (bf16[4,512,352]{1,2,0:T(8,128)(2,1)S(1)}, bf16[4,512,352]{1,2,0:T(8,128)(2,1)}, u32[]{:S(2)}) copy-start(bf16[4,512,352]{1,2,0:T(8,128)(2,1)} %param.30) | copy-start | bytes 4325380
  259.2 104.9 %all-gather.20.cloned.1.call-start = ((), (), s32[]{:S(2)}) async-start(), calls=%async_computation.14 | async-start | bytes 4456448 | tf_op jit(solution)/shard_map/all_gather | solution.py:62
  259.8 143.4 %all-gather.18.cloned.1.call-start = ((), (), s32[]{:S(2)}) async-start(), calls=%async_computation.13 | async-start | bytes 4456448 | tf_op jit(solution)/shard_map/all_gather | solution.py:62
  266.5 58.5 %copy-start.40 = (bf16[16,4,256]{2,0,1:T(8,128)(2,1)S(1)}, bf16[16,4,256]{2,0,1:T(8,128)(2,1)}, u32[]{:S(2)}) copy-start(bf16[16,4,256]{2,0,1:T(8,128)(2,1)} %get-tuple-element.34) | copy-start | bytes 98308
  324.9 144.6 %reduce-scatter.7.cloned.1.call-start = ((), (), s32[]{:S(2)}) async-start(), calls=%async_computation.7 | async-start | bytes 8912896 | tf_op jit(solution)/shard_map/reduce_scatter | solution.py:71
  343.2 196.2 %reduce-scatter.11.cloned.1.call-start = ((), (), s32[]{:S(2)}) async-start(), calls=%async_computation.9 | async-start | bytes 8912896 | tf_op jit(solution)/shard_map/reduce_scatter | solution.py:90
  371.0 35.9 %slice-start = ((s8[4325376]{0:T(1024)(128)(4,1)}), s8[131072]{0:T(1024)(128)(4,1)S(1)}, s32[]{:S(2)}) async-start(s8[4325376]{0:T(1024)(128)(4,1)} %bitcast.163), calls=%async_computation.15 | async-start | bytes 262144
  406.8 7.1 %copy-start.23 = (bf16[4,16,48,512]{3,2,1,0:T(8,128)(2,1)}, bf16[4,16,48,512]{3,2,1,0:T(8,128)(2,1)S(1)}, u32[]{:S(2)}) copy-start(bf16[4,16,48,512]{3,2,1,0:T(8,128)(2,1)S(1)} %copy.131) | copy-start | bytes 9437188
  430.5 15.8 %all-to-all-start.1 = ((f32[16,4,256]{2,1,0:T(4,128)}), f32[16,4,256]{2,1,0:T(4,128)S(1)}, u32[]{:S(2)}, u32[]{:S(2)}) async-start(f32[16,4,256]{2,1,0:T(4,128)} %get-tuple-element.12), calls=%async_computation.5 | async-start | bytes 131072 | tf_op jit(solution)/shard_map/all_to_all | solution.py:93
  434.9 5.6 %copy-start.22 = (bf16[4,16,48,512]{3,2,1,0:T(8,128)(2,1)S(1)}, bf16[4,16,48,512]{3,2,1,0:T(8,128)(2,1)}, u32[]{:S(2)}) copy-start(bf16[4,16,48,512]{3,2,1,0:T(8,128)(2,1)} %copy.127) | copy-start | bytes 9437188
  434.9 5.6 %copy-start.27 = (bf16[4,768,352]{1,2,0:T(8,128)(2,1)S(1)}, bf16[4,768,352]{1,2,0:T(8,128)(2,1)}, u32[]{:S(2)}) copy-start(bf16[4,768,352]{1,2,0:T(8,128)(2,1)} %get-tuple-element.23) | copy-start | bytes 6488068
  448.3 24.2 %copy-start.33 = (bf16[512,704]{0,1:T(8,128)(2,1)S(1)}, bf16[512,704]{0,1:T(8,128)(2,1)}, u32[]{:S(2)}) copy-start(bf16[512,704]{0,1:T(8,128)(2,1)} %param.27) | copy-start | bytes 2162692
  475.1 19.4 %all-to-all-start = ((f32[16,4,256]{2,1,0:T(4,128)}), f32[16,4,256]{2,1,0:T(4,128)S(1)}, u32[]{:S(2)}, u32[]{:S(2)}) async-start(f32[16,4,256]{2,1,0:T(4,128)} %get-tuple-element.14), calls=%async_computation.4 | async-start | bytes 131072 | tf_op jit(solution)/shard_map/all_to_all | solution.py:93
  483.1 5.6 %copy-start.24 = (bf16[4,16,48,512]{3,2,1,0:T(8,128)(2,1)S(1)}, bf16[4,16,48,512]{3,2,1,0:T(8,128)(2,1)}, u32[]{:S(2)}) copy-start(bf16[4,16,48,512]{3,2,1,0:T(8,128)(2,1)} %copy-done.23) | copy-start | bytes 9437188
  483.1 5.6 %copy-start.44 = (bf16[4,768,352]{1,2,0:T(8,128)(2,1)S(1)}, bf16[4,768,352]{1,2,0:T(8,128)(2,1)}, u32[]{:S(2)}) copy-start(bf16[4,768,352]{1,2,0:T(8,128)(2,1)} %get-tuple-element.21) | copy-start | bytes 6488068
  491.7 47.7 %copy-start.34 = (bf16[512,704]{0,1:T(8,128)(2,1)S(1)}, bf16[512,704]{0,1:T(8,128)(2,1)}, u32[]{:S(2)}) copy-start(bf16[512,704]{0,1:T(8,128)(2,1)} %param.28) | copy-start | bytes 2162692
  491.7 47.7 %copy-start.35 = (f32[256,704]{0,1:T(8,128)S(1)}, f32[256,704]{0,1:T(8,128)}, u32[]{:S(2)}) copy-start(f32[256,704]{0,1:T(8,128)} %fusion.104) | copy-start | bytes 2162692
  (34 other events, 93.4 us)
Sparse Core Ops, SparseCore 0:
  9.7 44.1 all-gather.11
  82.6 62.7 reduce-scatter.4
  147.0 40.5 all-gather.15
  189.7 36.8 all-gather.13
  259.3 62.4 reduce-scatter.8
  323.3 40.7 all-gather.19
  366.3 36.8 all-gather.17
  405.5 63.9 reduce-scatter.6
  471.9 67.4 reduce-scatter.10

commit v2 on v1

v2 whole, which is shorter than its diff:
```python
import functools

import jax
import jax.numpy as jnp
from jax import lax
from jax.experimental import pallas as pl
from jax.experimental.pallas import tpu as pltpu
from jax.sharding import PartitionSpec as P

F32 = jnp.float32
BF16 = jnp.bfloat16
MESH = pl.DeviceIdType.MESH
VMEM_BYTES = 66_900_000
TAB = 8


def slot_capacity(tokens, n_experts, top_k):
    return top_k * ((2 * tokens + n_experts - 1) // n_experts)


def dot(a, b):
    return jnp.dot(a, b, preferred_element_type=F32)


def dot_nt(a, b):
    return lax.dot_general(a, b, (((1,), (1,)), ((), ())), preferred_element_type=F32)


def dot_tn(a, b):
    return lax.dot_general(a, b, (((0,), (0,)), ((), ())), preferred_element_type=F32)


def swiglu_grads(pre_gate, pre_up, d_hidden):
    sigma = jax.nn.sigmoid(pre_gate)
    d_gate = d_hidden * pre_up * sigma * (1.0 + pre_gate * (1.0 - sigma))
    d_up = d_hidden * pre_gate * sigma
    return d_gate.astype(BF16), d_up.astype(BF16)


def hidden_of(rows, w_gate, w_up):
    pre_gate = dot_nt(rows, w_gate)
    pre_up = dot_nt(rows, w_up)
    return pre_gate, pre_up, (pre_gate * jax.nn.sigmoid(pre_gate) * pre_up).astype(BF16)


def when(cond, body):
    if isinstance(cond, bool):
        if cond:
            body()
    else:
        pl.when(cond)(body)


class Place:
    def __init__(self, nz):
        self.nz = nz
        self.me = lax.axis_index('ep')
        self.z = self.me // 2
        self.c = self.me % 2

    def chip(self, offset):
        return lax.rem(self.z + offset + 2 * self.nz, self.nz)

    def source(self, offset, rel):
        return self.chip(offset) * 2 + lax.rem(self.c + rel, 2)

    def device(self, offset, rel=0):
        return {'ep': self.source(offset, rel)}


class Gather:
    def __init__(self, place, buf, pieces, sems):
        self.p, self.buf, self.pieces = place, buf, pieces
        self.ss, self.rs, self.xs, self.xr = sems
        self.rows = buf.shape[1] // pieces

    def far(self, di, h):
        near = self.p.nz // 2 - 1
        return near + 1 if di == h else near

    def at(self, offset, rel, h):
        return self.buf.at[self.p.source(offset, rel), pl.ds(h * self.rows, self.rows)]

    def hop(self, di, h, k, offset):
        d = 1 - 2 * di
        ref = self.at(offset, 0, h)
        return pltpu.make_async_remote_copy(ref, ref, self.ss.at[di, h, k - 1], self.rs.at[di, h, k - 1],
                                            device_id=self.p.device(d), device_id_type=MESH)

    def send(self, di, h, k):
        d = 1 - 2 * di
        return self.hop(di, h, k, -d * (k - 1))

    def recv(self, di, h, k):
        d = 1 - 2 * di
        return self.hop(di, h, k, -d * k)

    def cross(self, h, offset, rel=0):
        ref = self.at(offset, rel, h)
        roff = lax.rem(offset + self.p.nz, self.p.nz) if not isinstance(offset, int) else offset % self.p.nz
        return pltpu.make_async_remote_copy(ref, ref, self.xs.at[roff, h], self.xr.at[roff, h],
                                            device_id=self.p.device(0, 1), device_id_type=MESH)

    def start(self):
        for h in range(self.pieces):
            for di in range(2):
                self.send(di, h, 1).start()
        for h in range(self.pieces):
            self.cross(h, 0).start()

    def step(self, k):
        for h in range(self.pieces):
            for di in range(2):
                d = 1 - 2 * di
                far = self.far(di, h)

                def arrive(di=di, h=h, d=d, far=far):
                    self.recv(di, h, k).wait_recv()
                    when(k + 1 <= far, lambda: self.send(di, h, k + 1).start())
                    self.cross(h, -d * k).start()

                when(k <= far, arrive)

    def wait_cross(self, offset):
        for h in range(self.pieces):
            self.cross(h, offset, 1).wait_recv()

    def drain(self):
        for h in range(self.pieces):
            for di in range(2):
                for k in range(1, self.far(di, h) + 1):
                    self.send(di, h, k).wait_send()
            for roff in range(self.p.nz):
                self.cross(h, roff).wait_send()


class Scatter:
    def __init__(self, place, acc, out, sib, box, sems):
        self.p, self.acc, self.out, self.sib, self.box = place, acc, out, sib, box
        self.xs, self.xr, self.ss, self.rs = sems
        self.half = acc.shape[1] // 2
        self.steps = place.nz - 1

    def cross(self, roff, slot):
        return pltpu.make_async_remote_copy(self.out.at[slot], self.sib.at[roff], self.xs.at[roff], self.xr.at[roff],
                                            device_id=self.p.device(0, 1), device_id_type=MESH)

    def merge(self, roff):
        self.cross(roff, 0).wait_recv()

        def add(i, carry):
            rows = pl.ds(i * 64, 64)
            self.acc[roff, rows, :] += self.sib[roff, rows, :]
            return carry

        lax.fori_loop(0, self.acc.shape[1] // 64, add, 0)

    def reach(self, i):
        return self.p.nz // 2 - (i + 1) // 2

    def roff(self, di, i):
        r = self.reach(i)
        return r if di == 0 else self.p.nz - r

    def side(self, di, i):
        return (i + di) % 2

    def hop(self, di, i):
        rows = pl.ds(self.side(di, i) * self.half, self.half)
        return pltpu.make_async_remote_copy(self.acc.at[self.roff(di, i), rows], self.box.at[di, i],
                                            self.ss.at[di, i], self.rs.at[di, i],
                                            device_id=self.p.device(1 - 2 * di), device_id_type=MESH)

    def take(self, di, i, roff):
        self.hop(di, i).wait_recv()
        first = self.side(di, i) * self.half

        def add(j, carry):
            rows = pl.ds(pl.multiple_of(first + j * 64, 64), 64)
            self.acc[roff, rows, :] += self.box[di, i, pl.ds(j * 64, 64), :]
            return carry

        lax.fori_loop(0, self.half // 64, add, 0)

    def step(self, i):
        for di in range(2):
            if isinstance(i, int) and i < 2:
                self.hop(di, i).start()
            else:
                self.take(di, i - 2, self.roff(di, i))
                self.hop(di, i).start()

    def finish(self):
        for i in (self.steps - 2, self.steps - 1):
            for di in range(2):
                self.take(di, i, 0)

    def drain(self):
        for i in range(self.steps):
            for di in range(2):
                self.hop(di, i).wait_send()


def stage_kernel(names, dims, fwd, bwd, layer, *refs):
    r = dict(zip(names, refs))
    nz, n_local, cap, tokens = dims
    p = Place(nz)
    n_dev = 2 * nz
    far = nz // 2
    slots = n_local * cap

    loads = [(r['x_in'], r['xg'].at[p.me], r['lsem'].at[0])]
    if bwd:
        loads.append((r['dy_in'], r['dg'].at[p.me], r['lsem'].at[1]))
        loads.append((r['tab_in'], r['tab'], r['lsem'].at[2]))
    else:
        loads.append((r['tab_in'], r['tab'].at[p.me], r['lsem'].at[2]))
    own = [pltpu.make_async_copy(*args) for args in loads]
    weights = [pltpu.make_async_copy(r[n + '_in'], r[n], r['wsem'].at[i])
               for i, n in enumerate(('ws1', 'ws3', 'ws2', 'w1', 'w3', 'w2'))]
    for copy in own + weights:
        copy.start()

    barrier = pltpu.get_barrier_semaphore()
    if bwd:
        for o in range(1, n_dev):
            pl.semaphore_signal(barrier, inc=1, device_id={'ep': lax.rem(p.me + o, n_dev)}, device_id_type=MESH)
        pl.semaphore_wait(barrier, n_dev - 1)
    else:
        for peer in (p.device(1), p.device(-1), p.device(0, 1)):
            pl.semaphore_signal(barrier, inc=1, device_id=peer, device_id_type=MESH)
        pl.semaphore_wait(barrier, 3)
    for copy in own:
        copy.wait()

    streams = []
    if not bwd:
        streams.append(Gather(p, r['tab'], 1, (r['ts'], r['tr'], r['txs'], r['txr'])))
    streams.append(Gather(p, r['xg'], 2, (r['gs'], r['gr'], r['gxs'], r['gxr'])))
    if bwd:
        streams.append(Gather(p, r['dg'], 2, (r['ds'], r['dr'], r['dxs'], r['dxr'])))
    for st in streams:
        st.start()

    tri = (lax.broadcasted_iota(jnp.int32, (tokens, tokens), 0)
           < lax.broadcasted_iota(jnp.int32, (tokens, tokens), 1))
    r['tri'][...] = jnp.where(tri, 1.0, 0.0).astype(BF16)

    for copy in weights[:3]:
        copy.wait()
    x_own = r['xg'][p.me]
    s_gate, s_up, s_hidden = hidden_of(x_own, r['ws1'][...], r['ws3'][...])
    if fwd:
        r['sh'][...] = dot(s_hidden, r['ws2'][...]) + x_own.astype(F32)
    if bwd:
        d_own = r['dg'][p.me]
        d_sg, d_su = swiglu_grads(s_gate, s_up, dot_nt(d_own, r['ws2'][...]))
        r['shd'][...] = dot(d_sg, r['ws1'][...]) + dot(d_su, r['ws3'][...]) + d_own.astype(F32)
    for copy in weights[3:]:
        copy.wait()

    sf = sb = None
    if fwd:
        sf = Scatter(p, r['facc'], r['fout'], r['fsib'], r['fbox'], (r['fxs'], r['fxr'], r['fss'], r['frs']))
    if bwd:
        sb = Scatter(p, r['bacc'], r['bout'], r['bsib'], r['bbox'], (r['bxs'], r['bxr'], r['bss'], r['brs']))

    def offset_of(k, q):
        sign = 1 - 2 * (q // 2)
        return k * sign

    def pos_rows(base, n):
        return pl.ds(pl.multiple_of(base * cap, 16), n * cap)

    def dispatch(k, base, n):
        def body(q, carry):
            s = p.source(offset_of(k, q), q % 2)
            ids = r['tab'][s, pl.ds(layer * TAB, TAB), :]
            gates = r['tab'][s, pl.ds((2 + layer) * TAB, TAB), :]
            used, gate = [], []
            for e in range(n_local):
                hit = ids == (p.me * n_local + e).astype(F32)
                used.append(jnp.max(jnp.where(hit, 1.0, 0.0), axis=0, keepdims=True))
                gate.append(jnp.sum(jnp.where(hit, gates, 0.0), axis=0, keepdims=True))
            zeros = jnp.zeros((8 - n_local, tokens), F32)
            used = jnp.concatenate(used + [zeros], axis=0)
            gate = jnp.concatenate(gate + [zeros], axis=0)
            rank = dot(used.astype(BF16), r['tri'][...])
            slot = jnp.where(used > 0, rank, -1.0)
            pos = base + q
            r['grow'][pos] = gate
            rows48 = lax.broadcasted_iota(jnp.int32, (cap, tokens), 0).astype(F32)
            for e in range(n_local):
                match = rows48 == slot[e:e + 1, :]
                r['pall'][pos, e * cap:(e + 1) * cap, :] = jnp.where(match, 1.0, 0.0).astype(BF16)
                if bwd:
                    col = jnp.sum(jnp.where(match, gate[e:e + 1, :], 0.0), axis=1, keepdims=True)
                    r['gcol'][e, pl.ds(pl.multiple_of(q * cap, 16), cap), :] = jnp.broadcast_to(col, (cap, 128))
            pick = r['pall'][pos]
            rows = dot(pick, r['xg'][s]).astype(BF16)
            for e in range(n_local):
                r['xr'][e, pos_rows(pos, 1), :] = rows[e * cap:(e + 1) * cap]
            if bwd:
                rows = dot(pick, r['dg'][s]).astype(BF16)
                for e in range(n_local):
                    r['dyr'][e, pos_rows(pos, 1), :] = rows[e * cap:(e + 1) * cap]
            return carry

        lax.fori_loop(0, n, body, 0)

    def expert_fwd(base, n):
        def body(e, carry):
            hidden = hidden_of(r['xr'][e, pos_rows(base, n), :], r['w1'][e], r['w3'][e])[2]
            r['rowbuf'][e, 0:n * cap, :] = dot(hidden, r['w2'][e]).astype(BF16)
            return carry

        lax.fori_loop(0, n_local, body, 0)

    def combine(k, base, n, sc, gated):
        for ridx in range(n // 2):
            offset = offset_of(k, 2 * ridx)
            roff = offset % nz if isinstance(offset, int) else lax.rem(offset + nz, nz)
            if not (isinstance(k, int) and k == 0):
                prev = k - 1
                if ridx == 0:
                    sc.cross(prev, 0).wait_send()
                else:
                    when(prev > 0, lambda: sc.cross(lax.rem(nz - prev, nz), 1).wait_send())
            for rel in (1, 0):
                q = 2 * ridx + rel
                pos = base + q
                rows = jnp.concatenate([r['rowbuf'][e, q * cap:(q + 1) * cap, :] for e in range(n_local)], axis=0)
                if gated:
                    pick = r['pall'][pos].astype(F32)
                    gate = r['grow'][pos]
                    part = None
                    for _ in range(3):
                        term = gate.astype(BF16).astype(F32)
                        gate = gate - term
                        wide = jnp.concatenate(
                            [pick[e * cap:(e + 1) * cap] * term[e:e + 1, :] for e in range(n_local)], axis=0)
                        one = dot_tn(wide.astype(BF16), rows)
                        part = one if part is None else part + one
                else:
                    part = dot_tn(r['pall'][pos], rows)
                if rel == 1:
                    sc.out[ridx] = part
                else:
                    sc.acc[roff] = part
            sc.cross(roff, ridx).start()

    def expert_bwd(base, n):
        def body(e, carry):
            span = pos_rows(base, n)
            here = slice(0, n * cap)
            pre_gate, pre_up, hidden = hidden_of(r['xr'][e, span, :], r['w1'][e], r['w3'][e])
            dy = r['dyr'][e, span, :]
            projected = dot_nt(dy, r['w2'][e])
            gcol = r['gcol'][e, here, 0:1]
            dgate = jnp.sum(hidden.astype(F32) * projected, axis=1, keepdims=True)
            r['gcol'][e, here, :] = jnp.broadcast_to(dgate, (n * cap, 128))
            r['dyr'][e, span, :] = (gcol * dy.astype(F32)).astype(BF16)
            da_gate, da_up = swiglu_grads(pre_gate, pre_up, gcol * projected)
            r['h'][e, span, :] = hidden
            r['da1'][e, span, :] = da_gate
            r['da3'][e, span, :] = da_up
            du = dot(da_gate, r['w1'][e]) + dot(da_up, r['w3'][e])
            r['rowbuf'][e, here, :] = du.astype(BF16)
            return carry

        lax.fori_loop(0, n_local, body, 0)

    def gate_rows(k, base, n):
        def body(q, carry):
            s = p.source(offset_of(k, q), q % 2)
            pos = base + q
            rows = []
            for e in range(n_local):
                col = r['gcol'][e, pl.ds(pl.multiple_of(q * cap, 16), cap), 0:1]
                pick = r['pall'][pos, e * cap:(e + 1) * cap, :].astype(F32)
                rows.append(jnp.sum(pick * col, axis=0, keepdims=True))
            wide = jnp.concatenate(rows, axis=0)
            half = tokens // 2
            r['dgout'][s] = jnp.concatenate([wide[:, :half], wide[:, half:]], axis=0)
            return carry

        lax.fori_loop(0, n, body, 0)

    def group(k, base, n, between=None):
        offsets = [offset_of(k, 2 * i) for i in range(n // 2)]
        for st in streams:
            for offset in offsets:
                st.wait_cross(offset)
        dispatch(k, base, n)
        if fwd:
            expert_fwd(base, n)
            combine(k, base, n, sf, True)
        if between is not None:
            between()
        if bwd:
            expert_bwd(base, n)
            combine(k, base, n, sb, False)
            gate_rows(k, base, n)

    def steps(k):
        for st in streams:
            st.step(k)

    def chain_start(sc):
        sc.merge(far)
        sc.step(0)
        sc.merge(far - 1)
        sc.merge(nz - far + 1)
        sc.step(1)

    group(0, 0, 2)

    def middle(k, carry):
        steps(k)
        group(k, 2 + (k - 1) * 4, 4)
        return carry

    lax.fori_loop(1, far, middle, 0)
    steps(far)
    group(far, n_dev - 2, 2, (lambda: chain_start(sf)) if fwd and bwd else None)
    if fwd and not bwd:
        chain_start(sf)
    if bwd:
        chain_start(sb)

    def grad_copy(o, wait):
        to = lax.rem(p.me + o, n_dev)
        landed = r['dgin'].at[lax.rem(p.me - o + n_dev, n_dev)] if wait else r['dgin'].at[p.me]
        return pltpu.make_async_remote_copy(r['dgout'].at[to], landed, r['as'].at[o], r['ar'].at[o],
                                            device_id={'ep': to}, device_id_type=MESH)

    if bwd:
        def push(o, carry):
            grad_copy(o, False).start()
            return carry

        lax.fori_loop(1, n_dev, push, 0)

    scatters = [sc for sc in (sf, sb) if sc is not None]

    def put(e):
        return [pltpu.make_async_copy(r['g' + n], r[n + '_out'].at[e], r['osem'].at[i])
                for i, n in enumerate(('dw1', 'dw3', 'dw2'))]

    def weight_grads(e):
        copies = put(e)

        @pl.when(e > 0)
        def _():
            for copy in copies:
                copy.wait()

        rows = r['xr'][e]
        r['gdw1'][...] = dot_tn(r['da1'][e], rows)
        r['gdw3'][...] = dot_tn(r['da3'][e], rows)
        r['gdw2'][...] = dot_tn(r['h'][e], r['dyr'][e])
        for copy in copies:
            copy.start()

    def ring(i, carry):
        for sc in scatters:
            @pl.when(i % 2 == 1)
            def _():
                sc.merge(sc.roff(0, i))
                sc.merge(sc.roff(1, i))
            sc.step(i)
        if bwd:
            @pl.when(i - 2 < n_local)
            def _():
                weight_grads(i - 2)
        return carry

    lax.fori_loop(2, nz - 1, ring, 0)
    for sc in scatters:
        sc.merge(0)
    if bwd:
        r['dgin'][p.me] = r['dgout'][p.me]

        def pull(o, carry):
            grad_copy(o, True).wait_recv()
            return carry

        lax.fori_loop(1, n_dev, pull, 0)
        ids = r['tab'][p.me, pl.ds(layer * TAB, TAB), :]

        def collect(dev, total):
            block = r['dgin'][dev]
            wide = jnp.concatenate([block[:n_local], block[n_local:]], axis=1)
            for e in range(n_local):
                total += jnp.where(ids == (dev * n_local + e).astype(F32), wide[e:e + 1, :], 0.0)
            return total

        r['dgate_out'][...] = lax.fori_loop(0, n_dev, collect, jnp.zeros((TAB, tokens), F32))
    if fwd:
        sf.finish()
        r['y_out'][...] = (r['sh'][...] + sf.acc[0]).astype(BF16)
    if bwd:
        sb.finish()
        r['dx_out'][...] = (r['shd'][...] + sb.acc[0]).astype(BF16)
        for copy in put(n_local - 1):
            copy.wait()

        def done(o, carry):
            grad_copy(o, False).wait_send()
            return carry

        lax.fori_loop(1, n_dev, done, 0)
    else:
        keep = pltpu.make_async_copy(r['tab'], r['tab_out'], r['osem'].at[0])
        keep.start()
        keep.wait()
    for st in streams:
        st.drain()
    for sc in scatters:
        sc.cross(far, 0).wait_send()
        sc.cross(nz - far + 1, 1).wait_send()
        sc.drain()


def stage(mesh_axis, dims, fwd, bwd, layer, x, dy, tab, weights, cid):
    nz, n_local, cap, tokens = dims
    n_dev = 2 * nz
    d = x.shape[1]
    w1, w3, w2, ws1, ws3, ws2 = weights
    f = w1.shape[1]
    slots = n_local * cap
    rows = n_dev * cap
    any_spec = pl.BlockSpec(memory_space=pl.ANY)
    vmem_spec = pl.BlockSpec(memory_space=pltpu.VMEM)
    dma = pltpu.SemaphoreType.DMA
    ins = {'x_in': x}
    if bwd:
        ins['dy_in'] = dy
    ins.update({'tab_in': tab, 'ws1_in': ws1, 'ws3_in': ws3, 'ws2_in': ws2, 'w1_in': w1, 'w3_in': w3, 'w2_in': w2})
    outs = {}
    if fwd:
        outs['y_out'] = ((tokens, d), BF16, vmem_spec)
    if bwd:
        outs['dx_out'] = ((tokens, d), BF16, vmem_spec)
        outs['dw1_out'] = (w1.shape, F32, any_spec)
        outs['dw3_out'] = (w3.shape, F32, any_spec)
        outs['dw2_out'] = (w2.shape, F32, any_spec)
        outs['dgate_out'] = ((TAB, tokens), F32, vmem_spec)
    else:
        outs['tab_out'] = ((n_dev,) + tab.shape, F32, any_spec)
    scratch = {
        'lsem': dma((3,)), 'wsem': dma((6,)), 'osem': dma((3,)),
        'xg': pltpu.VMEM((n_dev, tokens, d), BF16),
        'tab': pltpu.VMEM((n_dev, 4 * TAB, tokens), F32),
        'tri': pltpu.VMEM((tokens, tokens), BF16),
        'pall': pltpu.VMEM((n_dev, slots, tokens), BF16),
        'grow': pltpu.VMEM((n_dev, 8, tokens), F32),
        'xr': pltpu.VMEM((n_local, rows, d), BF16),
        'rowbuf': pltpu.VMEM((n_local, 4 * cap, d), BF16),
        'ws1': pltpu.VMEM(ws1.shape, BF16), 'ws3': pltpu.VMEM(ws3.shape, BF16), 'ws2': pltpu.VMEM(ws2.shape, BF16),
        'w1': pltpu.VMEM(w1.shape, BF16), 'w3': pltpu.VMEM(w3.shape, BF16), 'w2': pltpu.VMEM(w2.shape, BF16),
        'gs': dma((2, 2, nz // 2)), 'gr': dma((2, 2, nz // 2)), 'gxs': dma((nz, 2)), 'gxr': dma((nz, 2)),
    }
    if not bwd:
        scratch.update({'ts': dma((2, 1, nz // 2)), 'tr': dma((2, 1, nz // 2)), 'txs': dma((nz, 1)), 'txr': dma((nz, 1))})
    for on, tag in ((fwd, 'f'), (bwd, 'b')):
        if on:
            scratch.update({
                tag + 'acc': pltpu.VMEM((nz, tokens, d), F32),
                tag + 'out': pltpu.VMEM((2, tokens, d), F32),
                tag + 'sib': pltpu.VMEM((nz, tokens, d), F32),
                tag + 'box': pltpu.VMEM((2, nz - 1, tokens // 2, d), F32),
                tag + 'xs': dma((nz,)), tag + 'xr': dma((nz,)),
                tag + 'ss': dma((2, nz - 1)), tag + 'rs': dma((2, nz - 1)),
            })
    if fwd:
        scratch['sh'] = pltpu.VMEM((tokens, d), F32)
    if bwd:
        scratch.update({
            'dg': pltpu.VMEM((n_dev, tokens, d), BF16),
            'ds': dma((2, 2, nz // 2)), 'dr': dma((2, 2, nz // 2)), 'dxs': dma((nz, 2)), 'dxr': dma((nz, 2)),
            'shd': pltpu.VMEM((tokens, d), F32),
            'dyr': pltpu.VMEM((n_local, rows, d), BF16),
            'gcol': pltpu.VMEM((n_local, 4 * cap, 128), F32),
            'h': pltpu.VMEM((n_local, rows, f), BF16),
            'da1': pltpu.VMEM((n_local, rows, f), BF16),
            'da3': pltpu.VMEM((n_local, rows, f), BF16),
            'gdw1': pltpu.VMEM((f, d), F32), 'gdw3': pltpu.VMEM((f, d), F32), 'gdw2': pltpu.VMEM((f, d), F32),
            'dgout': pltpu.VMEM((n_dev, 2 * n_local, tokens // 2), F32),
            'dgin': pltpu.VMEM((n_dev, 2 * n_local, tokens // 2), F32),
            'as': dma((n_dev,)), 'ar': dma((n_dev,)),
        })
    names = list(ins) + list(outs) + list(scratch)
    result = pl.pallas_call(
        functools.partial(stage_kernel, names, dims, fwd, bwd, layer),
        out_shape=[jax.ShapeDtypeStruct(s, t) for s, t, _ in outs.values()],
        in_specs=[any_spec] * len(ins),
        out_specs=[spec for _, _, spec in outs.values()],
        scratch_shapes=list(scratch.values()),
        compiler_params=pltpu.CompilerParams(collective_id=cid, has_side_effects=True, vmem_limit_bytes=VMEM_BYTES),
        name='stage_' + ('f' if fwd else '') + ('b' if bwd else '') + '_ab'[1 + layer],
    )(*ins.values())
    return dict(zip(outs, result))


def solution(mesh):
    group_size = mesh.shape['ep']
    token_spec = P(('dp', 'ep'), None)
    expert_spec = P('ep', None, None)
    shared_spec = P(None, None)
    grad_spec = P(('dp', 'ep'), None, None)
    layer_specs = (expert_spec,) * 3 + (shared_spec,) * 3

    def device_step(x_in, d_out, idx_a, gate_a, idx_b, gate_b,
                    w1_a, w3_a, w2_a, ws1_a, ws3_a, ws2_a,
                    w1_b, w3_b, w2_b, ws1_b, ws3_b, ws2_b):
        def turned(w):
            return jnp.swapaxes(w, -1, -2)

        weights_a = (turned(w1_a), turned(w3_a), w2_a, turned(ws1_a), turned(ws3_a), ws2_a)
        weights_b = (turned(w1_b), turned(w3_b), w2_b, turned(ws1_b), turned(ws3_b), ws2_b)
        tokens, top_k = idx_a.shape
        n_local = w1_a.shape[0]
        dims = (group_size // 2, n_local, slot_capacity(tokens, n_local * group_size, top_k), tokens)

        def padded(values, fill):
            return jnp.pad(values.astype(F32), ((0, 0), (0, TAB - top_k)), constant_values=fill)

        table = jnp.concatenate([padded(idx_a, -1.0), padded(idx_b, -1.0), padded(gate_a, 0.0), padded(gate_b, 0.0)],
                                axis=1).T
        first = stage('ep', dims, True, False, 0, x_in, None, table, weights_a, 0)
        x_mid, tables = first['y_out'], first['tab_out']
        second = stage('ep', dims, True, True, 1, x_mid, d_out, tables, weights_b, 1)
        third = stage('ep', dims, False, True, 0, x_in, second['dx_out'], tables, weights_a, 2)
        return (second['y_out'], third['dx_out'],
                turned(third['dw1_out']), turned(third['dw3_out']), third['dw2_out'],
                turned(second['dw1_out']), turned(second['dw3_out']), second['dw2_out'],
                third['dgate_out'][:top_k].T, second['dgate_out'][:top_k].T)

    in_specs = (token_spec,) * 6 + layer_specs + layer_specs
    out_specs = (token_spec, token_spec) + (grad_spec,) * 6 + (token_spec, token_spec)
    return jax.shard_map(device_step, mesh=mesh, in_specs=in_specs, out_specs=out_specs, check_vma=False)
```

time: 560 us -> 367 us (0.66); the launches traced: 549 us -> 366 us
  Pallas kernels: 0 us -> 341 us
  waiting for transfers between devices: 320 us -> 0 us
  matrix products: 139 us -> 0 us
  blocking collectives: 24.2 us -> 0 us
  other arithmetic: 20.1 us -> 2.73 us
  between operations: 15 us -> 0.69 us
  starting transfers between devices: 13.8 us -> 0 us
    pallas_call x0 -> x3, Pallas kernels: none -> 341 us  [stage(): pl.pallas_call(functools.partial(stage_kernel, names, dims, fwd, bwd, lay...]
    reduce_scatter x4 -> x0, waiting for transfers between devices: 178 us -> none  [the longest x2 99.4 us: backward(): du_sum = lax.psum_scatter(part, 'ep', scatter_dimension=0, tiled=True)[0]]
    all_gather x5 -> x0, waiting for transfers between devices: 140 us -> none  [gather(): return lax.all_gather(rows, 'ep')]
    dot_general x46 -> x0, matrix products: 139 us -> none  [the longest x6 25.7 us: forward(): jnp.einsum('sect,escd->std', jnp.where(match, g[:, :, None, :], 0).astype...]
    all_gather x1 -> x0, blocking collectives: 24.2 us -> none  [gather(): return lax.all_gather(rows, 'ep')]
    convert_element_type x5 -> x2, other arithmetic: 13.8 us -> 1.4 us  [padded(): values.astype(F32)]
    all_to_all x2 -> x0, starting transfers between devices: 12.4 us -> none  [backward(): grad_back = lax.all_to_all(grad_tok, 'ep', 0, 0, tiled=True)]
    unnamed x94 -> x20, local copies, waits for them, and re-layouts: 13 us -> 20.2 us
  transfers between devices with their start and end apart: 11 -> 0, of which waited for: 9 -> 0; matrix products, arithmetic and copies ran while one was open for 20% -> 0% of each run, Pallas kernels for 0% -> 0%
where the time goes in v2:
time: 367 us; the launch traced here: 366 us
  Pallas kernels  341 us (93%)
  local copies, waits for them, and re-layouts  21.5 us (6%)
    pallas_call x3, Pallas kernels, stage(): pl.pallas_call(functools.partial(stage_kernel, names, dims, fwd, bwd, lay...  341 us
    unnamed x20, local copies, waits for them, and re-layouts  20.2 us

profile of v2, /device:TPU:21, one launch (start us, length us, event | category | flops | bytes accessed | tf_op | source)
XLA Modules:
  0.0 366.4 jit_solution(4381905518963186210)
XLA Ops:
  0.6 0.7 convert_element_type.6
  1.3 0.7 convert_element_type.7
  2.0 1.3 fusion.refs_1_
  3.4 91.7 %stage_fa.1 = (bf16[256,512]{1,0:T(8,128)(2,1)}, f32[16,32,256]{2,1,0:T(8,128)}) custom-call(bf16[256,512]{1,0:T(8,128)(2,1)} %refs_0_.3, f32[32,256]{1,0:T(8,128)} %fusion.refs_1_, bf16[704,512]{1,0:T(8,128)(2,1)} %bitcast.22, bf16[704,512]{1,0:T(8,128)(2,1)} %bitcast.24, bf16[704,512]{1,0:T(8,128)(2,1)} %refs_5_.3, bf16[4,352,512]{2,1,0:T(8,128)(2,1)} %bitcast.18, ...), custom_call_target="tpu_custom_call" | custom-call | tf_op jit(solution)/shard_map/stage_fa/pallas_call | solution.py:594
  95.1 147.8 %stage_fbb.1 = (bf16[256,512]{1,0:T(8,128)(2,1)}, bf16[256,512]{1,0:T(8,128)(2,1)}, f32[4,352,512]{2,1,0:T(8,128)}, f32[4,352,512]{2,1,0:T(8,128)}, f32[4,352,512]{2,1,0:T(8,128)}, /*index=5*/f32[8,256]{1,0:T(8,128)}) custom-call(bf16[256,512]{1,0:T(8,128)(2,1)} %get-tuple-element.23.refs_0_, bf16[256,512]{1,0:T(8,128)(2,1)} %refs_1_.1, ...), custom_call_target="tpu_custom_call" | custom-call | tf_op jit(solution)/shard_map/stage_fbb/pallas_call | solution.py:594
  242.9 0.0 copy-start.5
  242.9 102.0 %stage_ba.1 = (bf16[256,512]{1,0:T(8,128)(2,1)}, f32[4,352,512]{2,1,0:T(8,128)}, f32[4,352,512]{2,1,0:T(8,128)}, f32[4,352,512]{2,1,0:T(8,128)}, f32[8,256]{1,0:T(8,128)}) custom-call(bf16[256,512]{1,0:T(8,128)(2,1)} %refs_0_.3, bf16[256,512]{1,0:T(8,128)(2,1)} %get-tuple-element.26.refs_1_, f32[16,32,256]{2,1,0:T(8,128)} %get-tuple-element.24.refs_2_, ...), custom_call_target="tpu_custom_call" | custom-call | tf_op jit(solution)/shard_map/stage_ba/pallas_call | solution.py:594
  344.9 0.0 copy-done.5
  344.9 1.3 slice_bitcast_fusion
  346.2 1.7 copy.36
  347.9 1.7 copy.37
  349.5 0.0 copy-start.4
  349.5 3.8 %copy.38 = f32[4,512,352]{1,2,0:T(8,128)} copy(f32[4,512,352]{1,2,0:T(8,128)} %bitcast.29) | data formatting | bytes 5767168
  353.3 0.0 copy-done.4
  353.3 0.0 copy-start.3
  353.4 1.6 copy.39
  354.9 1.3 copy-done.3
  356.2 1.6 copy.40
  357.8 1.3 copy-done.2
  359.1 1.6 copy.41
  360.6 1.3 copy-done.1
  361.9 1.6 copy.42
  363.5 1.3 copy-done
  364.8 1.6 copy.43
  (3 shorter events, 0.0 us)
Async XLA Ops:
  242.9 102.0 %copy-start.5 = (f32[8,256]{1,0:T(8,128)S(1)}, f32[8,256]{1,0:T(8,128)}, u32[]{:S(2)}) copy-start(f32[8,256]{1,0:T(8,128)} %get-tuple-element.35) | copy-start | bytes 24580
  349.5 3.8 %copy-start.4 = (f32[4,352,512]{2,1,0:T(8,128)S(1)}, f32[4,352,512]{2,1,0:T(8,128)}, u32[]{:S(2)}) copy-start(f32[4,352,512]{2,1,0:T(8,128)} %get-tuple-element.29) | copy-start | bytes 8650756
  353.3 2.9 copy-start.3
  356.2 2.9 copy-start.2
  359.1 2.9 copy-start.1
  361.9 2.9 copy-start

commit v3 on v2

--- a/solution.py
+++ b/solution.py
@@ -182,13 +182,24 @@
 
         lax.fori_loop(0, self.half // 64, add, 0)
 
+    def begin(self, i):
+        for roff in sorted({self.roff(0, i), self.roff(1, i)}):
+            self.merge(roff)
+        for di in range(2):
+            self.hop(di, i).start()
+
     def step(self, i):
         for di in range(2):
-            if isinstance(i, int) and i < 2:
-                self.hop(di, i).start()
-            else:
-                self.take(di, i - 2, self.roff(di, i))
-                self.hop(di, i).start()
+            self.take(di, i - 2, self.roff(di, i))
+            self.hop(di, i).start()
+
+    def merge_for(self, i):
+        self.merge(self.roff(0, i))
+        self.merge(self.roff(1, i))
+
+    def free(self, frees):
+        for slot, roff, cond in frees:
+            when(cond, functools.partial(lambda slot, roff: self.cross(roff, slot).wait_send(), slot, roff))
 
     def finish(self):
         for i in (self.steps - 2, self.steps - 1):
@@ -237,8 +248,10 @@
     if not bwd:
         streams.append(Gather(p, r['tab'], 1, (r['ts'], r['tr'], r['txs'], r['txr'])))
     streams.append(Gather(p, r['xg'], 2, (r['gs'], r['gr'], r['gxs'], r['gxr'])))
-    if bwd:
-        streams.append(Gather(p, r['dg'], 2, (r['ds'], r['dr'], r['dxs'], r['dxr'])))
+    x_streams, dy_stream = list(streams), None
+    if bwd:
+        dy_stream = Gather(p, r['dg'], 2, (r['ds'], r['dr'], r['dxs'], r['dxr']))
+        streams.append(dy_stream)
     for st in streams:
         st.start()
 
@@ -293,17 +306,25 @@
             for e in range(n_local):
                 match = rows48 == slot[e:e + 1, :]
                 r['pall'][pos, e * cap:(e + 1) * cap, :] = jnp.where(match, 1.0, 0.0).astype(BF16)
-                if bwd:
-                    col = jnp.sum(jnp.where(match, gate[e:e + 1, :], 0.0), axis=1, keepdims=True)
-                    r['gcol'][e, pl.ds(pl.multiple_of(q * cap, 16), cap), :] = jnp.broadcast_to(col, (cap, 128))
-            pick = r['pall'][pos]
-            rows = dot(pick, r['xg'][s]).astype(BF16)
+            rows = dot(r['pall'][pos], r['xg'][s]).astype(BF16)
             for e in range(n_local):
                 r['xr'][e, pos_rows(pos, 1), :] = rows[e * cap:(e + 1) * cap]
-            if bwd:
-                rows = dot(pick, r['dg'][s]).astype(BF16)
-                for e in range(n_local):
-                    r['dyr'][e, pos_rows(pos, 1), :] = rows[e * cap:(e + 1) * cap]
+            return carry
+
+        lax.fori_loop(0, n, body, 0)
+
+    def dispatch_dy(k, base, n):
+        def body(q, carry):
+            s = p.source(offset_of(k, q), q % 2)
+            pos = base + q
+            pick = r['pall'][pos]
+            gate = r['grow'][pos]
+            rows = dot(pick, r['dg'][s]).astype(BF16)
+            for e in range(n_local):
+                wide = pick[e * cap:(e + 1) * cap].astype(F32) * gate[e:e + 1, :]
+                col = jnp.sum(wide, axis=1, keepdims=True)
+                r['gcol'][e, pl.ds(pl.multiple_of(q * cap, 16), cap), :] = jnp.broadcast_to(col, (cap, 128))
+                r['dyr'][e, pos_rows(pos, 1), :] = rows[e * cap:(e + 1) * cap]
             return carry
 
         lax.fori_loop(0, n, body, 0)
@@ -316,16 +337,11 @@
 
         lax.fori_loop(0, n_local, body, 0)
 
-    def combine(k, base, n, sc, gated):
+    def combine(k, base, n, sc, gated, frees):
+        sc.free(frees)
         for ridx in range(n // 2):
             offset = offset_of(k, 2 * ridx)
             roff = offset % nz if isinstance(offset, int) else lax.rem(offset + nz, nz)
-            if not (isinstance(k, int) and k == 0):
-                prev = k - 1
-                if ridx == 0:
-                    sc.cross(prev, 0).wait_send()
-                else:
-                    when(prev > 0, lambda: sc.cross(lax.rem(nz - prev, nz), 1).wait_send())
             for rel in (1, 0):
                 q = 2 * ridx + rel
                 pos = base + q
@@ -386,47 +402,62 @@
 
         lax.fori_loop(0, n, body, 0)
 
-    def group(k, base, n, between=None):
-        offsets = [offset_of(k, 2 * i) for i in range(n // 2)]
-        for st in streams:
-            for offset in offsets:
-                st.wait_cross(offset)
+    def spot(k):
+        if isinstance(k, int) and k in (0, far):
+            return (0 if k == 0 else n_dev - 2), 2
+        return 2 + (k - 1) * 4, 4
+
+    def arrived(st, k, n):
+        for i in range(n // 2):
+            st.wait_cross(offset_of(k, 2 * i))
+
+    def group_x(k, frees):
+        base, n = spot(k)
+        for st in x_streams:
+            arrived(st, k, n)
         dispatch(k, base, n)
         if fwd:
             expert_fwd(base, n)
-            combine(k, base, n, sf, True)
-        if between is not None:
-            between()
-        if bwd:
-            expert_bwd(base, n)
-            combine(k, base, n, sb, False)
-            gate_rows(k, base, n)
+            combine(k, base, n, sf, True, frees)
+
+    def group_dy(k, frees):
+        base, n = spot(k)
+        arrived(dy_stream, k, n)
+        dispatch_dy(k, base, n)
+        expert_bwd(base, n)
+        combine(k, base, n, sb, False, frees)
+        gate_rows(k, base, n)
 
     def steps(k):
         for st in streams:
             st.step(k)
 
-    def chain_start(sc):
-        sc.merge(far)
-        sc.step(0)
-        sc.merge(far - 1)
-        sc.merge(nz - far + 1)
-        sc.step(1)
-
-    group(0, 0, 2)
+    def upward(k, first):
+        return [(0, k - 1, k > first), (1, lax.rem(nz - (k - 1), nz), k > max(first, 1))]
+
+    first = 0 if bwd else 1
+    if bwd:
+        group_x(0, [])
+        if not fwd:
+            group_dy(0, [])
 
     def middle(k, carry):
         steps(k)
-        group(k, 2 + (k - 1) * 4, 4)
+        group_x(k, upward(k, first))
+        if not fwd:
+            group_dy(k, upward(k, first))
         return carry
 
     lax.fori_loop(1, far, middle, 0)
     steps(far)
-    group(far, n_dev - 2, 2, (lambda: chain_start(sf)) if fwd and bwd else None)
-    if fwd and not bwd:
-        chain_start(sf)
-    if bwd:
-        chain_start(sb)
+    lead = sf if fwd else sb
+    lead.begin(1)
+    last = [(0, far - 1, True)]
+    group_x(far, last)
+    if not fwd:
+        group_dy(far, last)
+    lead.begin(0)
+    left = [(lead, 0, far), (lead, 1, nz - far + 1)]
 
     def grad_copy(o, wait):
         to = lax.rem(p.me + o, n_dev)
@@ -434,12 +465,9 @@
         return pltpu.make_async_remote_copy(r['dgout'].at[to], landed, r['as'].at[o], r['ar'].at[o],
                                             device_id={'ep': to}, device_id_type=MESH)
 
-    if bwd:
-        def push(o, carry):
-            grad_copy(o, False).start()
-            return carry
-
-        lax.fori_loop(1, n_dev, push, 0)
+    def push(o, carry):
+        grad_copy(o, False).start()
+        return carry
 
     scatters = [sc for sc in (sf, sb) if sc is not None]
 
@@ -462,20 +490,50 @@
         for copy in copies:
             copy.start()
 
-    def ring(i, carry):
-        for sc in scatters:
-            @pl.when(i % 2 == 1)
-            def _():
-                sc.merge(sc.roff(0, i))
-                sc.merge(sc.roff(1, i))
-            sc.step(i)
-        if bwd:
-            @pl.when(i - 2 < n_local)
-            def _():
-                weight_grads(i - 2)
-        return carry
-
-    lax.fori_loop(2, nz - 1, ring, 0)
+    def order(j):
+        return 3 + 2 * (j // 2) - j % 2
+
+    def turn(sc, j):
+        i = order(j)
+        when(j % 2 == 0, lambda: sc.merge_for(i))
+        sc.step(i)
+
+    turns = nz - 4
+    if not bwd:
+        turn(sf, 0)
+        group_x(0, [(0, far, True)])
+        left[0] = (sf, 0, 0)
+        for j in range(1, turns):
+            turn(sf, j)
+        sf.step(nz - 2)
+    else:
+        if fwd:
+            group_dy(far, [])
+            turn(sf, 0)
+            group_dy(far - 1, [(0, far, True)])
+            turn(sf, 1)
+            sb.begin(1)
+            sb.begin(0)
+
+            def outward(j, carry):
+                k = far - j
+                group_dy(k, [(0, k + 1, True), (1, nz - (k + 1), True)])
+                turn(sf, j)
+                return carry
+
+            lax.fori_loop(2, far, outward, 0)
+            group_dy(0, [(0, 1, True)])
+            left += [(sb, 0, 0), (sb, 1, nz - 1)]
+            sf.step(nz - 2)
+        lax.fori_loop(1, n_dev, push, 0)
+
+        def ring(j, carry):
+            turn(sb, j)
+            weight_grads(j)
+            return carry
+
+        lax.fori_loop(0, turns, ring, 0)
+        sb.step(nz - 2)
     for sc in scatters:
         sc.merge(0)
     if bwd:
@@ -516,9 +574,9 @@
         keep.wait()
     for st in streams:
         st.drain()
+    for sc, slot, roff in left:
+        sc.cross(roff, slot).wait_send()
     for sc in scatters:
-        sc.cross(far, 0).wait_send()
-        sc.cross(nz - far + 1, 1).wait_send()
         sc.drain()
 
 
@@ -603,6 +661,42 @@
     return dict(zip(outs, result))
 
 
+def settle_kernel(pieces, *refs):
+    n = len(refs[:-2]) // 3
+    ins, outs, bufs = refs[:n], refs[n:2 * n], refs[2 * n:3 * n]
+    get_sem, put_sem = refs[-2:]
+    gets, puts = [], []
+    for i in range(n):
+        for j in range(pieces[i]):
+            rows = pl.ds(j * (ins[i].shape[0] // pieces[i]), ins[i].shape[0] // pieces[i])
+            at = len(gets)
+            gets.append(pltpu.make_async_copy(ins[i].at[rows], bufs[i].at[rows], get_sem.at[at]))
+            puts.append(pltpu.make_async_copy(bufs[i].at[rows], outs[i].at[rows], put_sem.at[at]))
+    for get in gets:
+        get.start()
+    for get, put in zip(gets, puts):
+        get.wait()
+        put.start()
+    for put in puts:
+        put.wait()
+
+
+def settle(arrays):
+    pieces = [a.shape[0] if a.ndim == 3 else 1 for a in arrays]
+    total = sum(pieces)
+    any_spec = pl.BlockSpec(memory_space=pl.ANY)
+    return pl.pallas_call(
+        functools.partial(settle_kernel, pieces),
+        out_shape=[jax.ShapeDtypeStruct(a.shape, a.dtype) for a in arrays],
+        in_specs=[any_spec] * len(arrays),
+        out_specs=[any_spec] * len(arrays),
+        scratch_shapes=[pltpu.VMEM(a.shape, a.dtype) for a in arrays]
+        + [pltpu.SemaphoreType.DMA((total,)), pltpu.SemaphoreType.DMA((total,))],
+        compiler_params=pltpu.CompilerParams(vmem_limit_bytes=VMEM_BYTES),
+        name='settle',
+    )(*arrays)
+
+
 def solution(mesh):
     group_size = mesh.shape['ep']
     token_spec = P(('dp', 'ep'), None)
@@ -632,10 +726,12 @@
         x_mid, tables = first['y_out'], first['tab_out']
         second = stage('ep', dims, True, True, 1, x_mid, d_out, tables, weights_b, 1)
         third = stage('ep', dims, False, True, 0, x_in, second['dx_out'], tables, weights_a, 2)
-        return (second['y_out'], third['dx_out'],
-                turned(third['dw1_out']), turned(third['dw3_out']), third['dw2_out'],
-                turned(second['dw1_out']), turned(second['dw3_out']), second['dw2_out'],
-                third['dgate_out'][:top_k].T, second['dgate_out'][:top_k].T)
+        x_last, d_first, *grads = settle(
+            [second['y_out'], third['dx_out']]
+            + [layer[n] for layer in (third, second) for n in ('dw1_out', 'dw3_out', 'dw2_out')])
+        for at in (0, 1, 3, 4):
+            grads[at] = turned(grads[at])
+        return (x_last, d_first, *grads, third['dgate_out'][:top_k].T, second['dgate_out'][:top_k].T)
 
     in_specs = (token_spec,) * 6 + layer_specs + layer_specs
     out_specs = (token_spec, token_spec) + (grad_spec,) * 6 + (token_spec, token_spec)

time: 367 us -> 336 us (0.916)
  local copies, waits for them, and re-layouts: 21.5 us -> 0.61 us
  Pallas kernels: 341 us -> 332 us
    pallas_call x3, Pallas kernels: 341 us -> 319 us  [stage(): pl.pallas_call(functools.partial(stage_kernel, names, dims, fwd, bwd, lay...]
    unnamed x20 -> x4, local copies, waits for them, and re-layouts: 20.2 us -> 0.01 us
    pallas_call x0 -> x1, Pallas kernels: none -> 13 us  [settle(): pl.pallas_call(functools.partial(settle_kernel, pieces), out_shape=[jax.S...]
where the time goes in v3:
time: 336 us
  Pallas kernels  332 us (99%)
    pallas_call x3, Pallas kernels, stage(): pl.pallas_call(functools.partial(stage_kernel, names, dims, fwd, bwd, lay...  319 us
    pallas_call x1, Pallas kernels, settle(): pl.pallas_call(functools.partial(settle_kernel, pieces), out_shape=[jax.S...  13 us

profile of v3, /device:TPU:21, one launch (start us, length us, event | category | flops | bytes accessed | tf_op | source)
XLA Modules:
  0.0 335.8 jit_solution(7563967426254203622)
XLA Ops:
  0.6 0.7 convert_element_type.6
  1.3 0.7 convert_element_type.7
  2.0 1.3 fusion.refs_1_
  3.4 87.8 %stage_fa.1 = (bf16[256,512]{1,0:T(8,128)(2,1)}, f32[16,32,256]{2,1,0:T(8,128)}) custom-call(bf16[256,512]{1,0:T(8,128)(2,1)} %refs_0_.3, f32[32,256]{1,0:T(8,128)} %fusion.refs_1_, bf16[704,512]{1,0:T(8,128)(2,1)} %bitcast.22, bf16[704,512]{1,0:T(8,128)(2,1)} %bitcast.24, bf16[704,512]{1,0:T(8,128)(2,1)} %refs_5_.3, bf16[4,352,512]{2,1,0:T(8,128)(2,1)} %bitcast.18, ...), custom_call_target="tpu_custom_call" | custom-call | tf_op jit(solution)/shard_map/stage_fa/pallas_call | solution.py:652
  91.2 131.3 %stage_fbb.1 = (bf16[256,512]{1,0:T(8,128)(2,1)}, bf16[256,512]{1,0:T(8,128)(2,1)}, f32[4,352,512]{2,1,0:T(8,128)}, f32[4,352,512]{2,1,0:T(8,128)}, f32[4,352,512]{2,1,0:T(8,128)}, /*index=5*/f32[8,256]{1,0:T(8,128)}) custom-call(bf16[256,512]{1,0:T(8,128)(2,1)} %get-tuple-element.31.refs_0_, bf16[256,512]{1,0:T(8,128)(2,1)} %refs_1_.1, ...), custom_call_target="tpu_custom_call" | custom-call | tf_op jit(solution)/shard_map/stage_fbb/pallas_call | solution.py:652
  222.5 99.7 %stage_ba.1 = (bf16[256,512]{1,0:T(8,128)(2,1)}, f32[4,352,512]{2,1,0:T(8,128)}, f32[4,352,512]{2,1,0:T(8,128)}, f32[4,352,512]{2,1,0:T(8,128)}, f32[8,256]{1,0:T(8,128)}) custom-call(bf16[256,512]{1,0:T(8,128)(2,1)} %refs_0_.3, bf16[256,512]{1,0:T(8,128)(2,1)} %get-tuple-element.34.refs_1_, f32[16,32,256]{2,1,0:T(8,128)} %get-tuple-element.32.refs_2_, ...), custom_call_target="tpu_custom_call" | custom-call | tf_op jit(solution)/shard_map/stage_ba/pallas_call | solution.py:652
  322.2 0.0 copy-start
  322.2 0.0 copy-start.1
  322.2 13.0 %settle.1 = (bf16[256,512]{1,0:T(8,128)(2,1)}, bf16[256,512]{1,0:T(8,128)(2,1)}, f32[4,352,512]{2,1,0:T(8,128)}, f32[4,352,512]{2,1,0:T(8,128)}, f32[4,352,512]{...) custom-call(bf16[256,512]{1,0:T(8,128)(2,1)} %get-tuple-element.33.refs_0_, ...), custom_call_target="tpu_custom_call" | custom-call | tf_op jit(solution)/shard_map/settle/pallas_call | solution.py:688
  335.2 0.0 copy-done
  335.2 0.0 copy-done.1
  335.2 0.6 slice_bitcast_fusion
Async XLA Ops:
  322.2 13.0 %copy-start = (f32[8,256]{1,0:T(8,128)S(1)}, f32[8,256]{1,0:T(8,128)}, u32[]{:S(2)}) copy-start(f32[8,256]{1,0:T(8,128)} %get-tuple-element.51) | copy-start | bytes 24580
  322.2 13.0 %copy-start.1 = (f32[8,256]{1,0:T(8,128)S(1)}, f32[8,256]{1,0:T(8,128)}, u32[]{:S(2)}) copy-start(f32[8,256]{1,0:T(8,128)} %get-tuple-element.50) | copy-start | bytes 24580

commit v4 on v3

v4 whole, which is shorter than its diff:
```python
import functools

import jax
import jax.numpy as jnp
from jax import lax
from jax.experimental import pallas as pl
from jax.experimental.pallas import tpu as pltpu
from jax.sharding import PartitionSpec as P

F32 = jnp.float32
BF16 = jnp.bfloat16
MESH = pl.DeviceIdType.MESH
VMEM_BYTES = 67_000_000
TAB = 8


def slot_capacity(tokens, n_experts, top_k):
    return top_k * ((2 * tokens + n_experts - 1) // n_experts)


def dot(a, b):
    return jnp.dot(a, b, preferred_element_type=F32)


def dot_nt(a, b):
    return lax.dot_general(a, b, (((1,), (1,)), ((), ())), preferred_element_type=F32)


def dot_tn(a, b):
    return lax.dot_general(a, b, (((0,), (0,)), ((), ())), preferred_element_type=F32)


def swiglu_grads(pre_gate, pre_up, d_hidden):
    sigma = jax.nn.sigmoid(pre_gate)
    d_gate = d_hidden * pre_up * sigma * (1.0 + pre_gate * (1.0 - sigma))
    d_up = d_hidden * pre_gate * sigma
    return d_gate.astype(BF16), d_up.astype(BF16)


def hidden_of(rows, w_gate, w_up):
    pre_gate = dot_nt(rows, w_gate)
    pre_up = dot_nt(rows, w_up)
    return pre_gate, pre_up, (pre_gate * jax.nn.sigmoid(pre_gate) * pre_up).astype(BF16)


def when(cond, body):
    if isinstance(cond, bool):
        if cond:
            body()
    else:
        pl.when(cond)(body)


class Place:
    def __init__(self, nz):
        self.nz = nz
        self.me = lax.axis_index('ep')
        self.z = self.me // 2
        self.c = self.me % 2

    def chip(self, offset):
        return lax.rem(self.z + offset + 2 * self.nz, self.nz)

    def source(self, offset, rel):
        return self.chip(offset) * 2 + lax.rem(self.c + rel, 2)

    def device(self, offset, rel=0):
        return {'ep': self.source(offset, rel)}


class Gather:
    def __init__(self, place, buf, pieces, sems):
        self.p, self.buf, self.pieces = place, buf, pieces
        self.ss, self.rs, self.xs, self.xr = sems
        self.rows = buf.shape[1] // pieces

    def far(self, di, h):
        near = self.p.nz // 2 - 1
        return near + 1 if di == h else near

    def at(self, offset, rel, h):
        return self.buf.at[self.p.source(offset, rel), pl.ds(h * self.rows, self.rows)]

    def hop(self, di, h, k, offset):
        d = 1 - 2 * di
        ref = self.at(offset, 0, h)
        return pltpu.make_async_remote_copy(ref, ref, self.ss.at[di, h, k - 1], self.rs.at[di, h, k - 1],
                                            device_id=self.p.device(d), device_id_type=MESH)

    def send(self, di, h, k):
        d = 1 - 2 * di
        return self.hop(di, h, k, -d * (k - 1))

    def recv(self, di, h, k):
        d = 1 - 2 * di
        return self.hop(di, h, k, -d * k)

    def cross(self, h, offset, rel=0):
        ref = self.at(offset, rel, h)
        roff = lax.rem(offset + self.p.nz, self.p.nz) if not isinstance(offset, int) else offset % self.p.nz
        return pltpu.make_async_remote_copy(ref, ref, self.xs.at[roff, h], self.xr.at[roff, h],
                                            device_id=self.p.device(0, 1), device_id_type=MESH)

    def start(self):
        for h in range(self.pieces):
            for di in range(2):
                self.send(di, h, 1).start()
        for h in range(self.pieces):
            self.cross(h, 0).start()

    def step(self, k):
        for h in range(self.pieces):
            for di in range(2):
                d = 1 - 2 * di
                far = self.far(di, h)

                def arrive(di=di, h=h, d=d, far=far):
                    self.recv(di, h, k).wait_recv()
                    when(k + 1 <= far, lambda: self.send(di, h, k + 1).start())
                    self.cross(h, -d * k).start()

                when(k <= far, arrive)

    def wait_cross(self, offset):
        for h in range(self.pieces):
            self.cross(h, offset, 1).wait_recv()

    def drain(self):
        for h in range(self.pieces):
            for di in range(2):
                for k in range(1, self.far(di, h) + 1):
                    self.send(di, h, k).wait_send()
            for roff in range(self.p.nz):
                self.cross(h, roff).wait_send()


class Scatter:
    def __init__(self, place, acc, out, sib, box, sems):
        self.p, self.acc, self.out, self.sib, self.box = place, acc, out, sib, box
        self.xs, self.xr, self.ss, self.rs = sems
        self.half = acc.shape[1] // 2
        self.steps = place.nz - 1

    def cross(self, roff, slot):
        return pltpu.make_async_remote_copy(self.out.at[slot], self.sib.at[roff], self.xs.at[roff], self.xr.at[roff],
                                            device_id=self.p.device(0, 1), device_id_type=MESH)

    def merge(self, roff):
        self.cross(roff, 0).wait_recv()

        def add(i, carry):
            rows = pl.ds(i * 64, 64)
            self.acc[roff, rows, :] += self.sib[roff, rows, :]
            return carry

        lax.fori_loop(0, self.acc.shape[1] // 64, add, 0)

    def reach(self, i):
        return self.p.nz // 2 - (i + 1) // 2

    def roff(self, di, i):
        r = self.reach(i)
        return r if di == 0 else self.p.nz - r

    def side(self, di, i):
        return (i + di) % 2

    def hop(self, di, i):
        rows = pl.ds(self.side(di, i) * self.half, self.half)
        return pltpu.make_async_remote_copy(self.acc.at[self.roff(di, i), rows], self.box.at[di, i],
                                            self.ss.at[di, i], self.rs.at[di, i],
                                            device_id=self.p.device(1 - 2 * di), device_id_type=MESH)

    def take(self, di, i, roff):
        self.hop(di, i).wait_recv()
        first = self.side(di, i) * self.half

        def add(j, carry):
            rows = pl.ds(pl.multiple_of(first + j * 64, 64), 64)
            self.acc[roff, rows, :] += self.box[di, i, pl.ds(j * 64, 64), :]
            return carry

        lax.fori_loop(0, self.half // 64, add, 0)

    def begin(self, i):
        for roff in sorted({self.roff(0, i), self.roff(1, i)}):
            self.merge(roff)
        for di in range(2):
            self.hop(di, i).start()

    def step(self, i):
        for di in range(2):
            self.take(di, i - 2, self.roff(di, i))
            self.hop(di, i).start()

    def merge_for(self, i):
        self.merge(self.roff(0, i))
        self.merge(self.roff(1, i))

    def free(self, frees):
        for slot, roff, cond in frees:
            when(cond, functools.partial(lambda slot, roff: self.cross(roff, slot).wait_send(), slot, roff))

    def finish(self):
        for i in (self.steps - 2, self.steps - 1):
            for di in range(2):
                self.take(di, i, 0)

    def drain(self):
        for i in range(self.steps):
            for di in range(2):
                self.hop(di, i).wait_send()


def step_kernel(names, dims, *refs):
    r = dict(zip(names, refs))
    nz, n_local, cap, tokens = dims
    p = Place(nz)
    n_dev = 2 * nz
    far = nz // 2

    def load_weights(tag):
        return [pltpu.make_async_copy(r[n + tag], r[n], r['wsem'].at[i])
                for i, n in enumerate(('ws1', 'ws3', 'ws2', 'w1', 'w3', 'w2'))]

    def load_own(name, buf, i):
        return pltpu.make_async_copy(r[name], r[buf].at[p.me], r['lsem'].at[i])

    own = [load_own('tab_in', 'tab', 0), load_own('x_in', 'xg', 1)]
    own_dy = load_own('dy_in', 'dg', 2)
    for copy in own + [own_dy]:
        copy.start()

    barrier = pltpu.get_barrier_semaphore()
    for o in range(1, n_dev):
        pl.semaphore_signal(barrier, inc=1, device_id={'ep': lax.rem(p.me + o, n_dev)}, device_id_type=MESH)
    pl.semaphore_wait(barrier, n_dev - 1)

    tabs = Gather(p, r['tab'], 1, (r['ts'], r['tr'], r['txs'], r['txr']))
    xs = Gather(p, r['xg'], 2, (r['gs'], r['gr'], r['gxs'], r['gxr']))
    ds = Gather(p, r['dg'], 2, (r['ds'], r['dr'], r['dxs'], r['dxr']))
    sf = Scatter(p, r['facc'], r['fout'], r['fsib'], r['fbox'], (r['fxs'], r['fxr'], r['fss'], r['frs']))
    sb = Scatter(p, r['bacc'], r['bout'], r['bsib'], r['bbox'], (r['bxs'], r['bxr'], r['bss'], r['brs']))

    for copy in own:
        copy.wait()
    tabs.start()
    xs.start()

    tri = (lax.broadcasted_iota(jnp.int32, (tokens, tokens), 0)
           < lax.broadcasted_iota(jnp.int32, (tokens, tokens), 1))
    r['tri'][...] = jnp.where(tri, 1.0, 0.0).astype(BF16)

    def offset_of(k, q):
        return k * (1 - 2 * (q // 2))

    def pos_rows(base, n):
        return pl.ds(pl.multiple_of(base * cap, 16), n * cap)

    def spot(k):
        if isinstance(k, int) and k in (0, far):
            return (0 if k == 0 else n_dev - 2), 2
        return 2 + (k - 1) * 4, 4

    def arrived(st, k):
        for i in range(spot(k)[1] // 2):
            st.wait_cross(offset_of(k, 2 * i))

    def route(k, layer):
        base, n = spot(k)

        def body(q, carry):
            s = p.source(offset_of(k, q), q % 2)
            ids = r['tab'][s, pl.ds(layer * TAB, TAB), :]
            gates = r['tab'][s, pl.ds((2 + layer) * TAB, TAB), :]
            used, gate = [], []
            for e in range(n_local):
                hit = ids == (p.me * n_local + e).astype(F32)
                used.append(jnp.max(jnp.where(hit, 1.0, 0.0), axis=0, keepdims=True))
                gate.append(jnp.sum(jnp.where(hit, gates, 0.0), axis=0, keepdims=True))
            zeros = jnp.zeros((8 - n_local, tokens), F32)
            used = jnp.concatenate(used + [zeros], axis=0)
            rank = dot(used.astype(BF16), r['tri'][...])
            slot = jnp.where(used > 0, rank, -1.0)
            pos = base + q
            r['grow'][pos] = jnp.concatenate(gate + [zeros], axis=0)
            place = lax.broadcasted_iota(jnp.int32, (cap, tokens), 0).astype(F32)
            for e in range(n_local):
                r['pall'][pos, e * cap:(e + 1) * cap, :] = jnp.where(place == slot[e:e + 1, :], 1.0, 0.0).astype(BF16)
            return carry

        lax.fori_loop(0, n, body, 0)

    def dispatch(k):
        base, n = spot(k)

        def body(q, carry):
            s = p.source(offset_of(k, q), q % 2)
            pos = base + q
            rows = dot(r['pall'][pos], r['xg'][s]).astype(BF16)
            for e in range(n_local):
                r['xr'][e, pos_rows(pos, 1), :] = rows[e * cap:(e + 1) * cap]
            return carry

        lax.fori_loop(0, n, body, 0)

    def dispatch_dy(k):
        base, n = spot(k)

        def body(q, carry):
            s = p.source(offset_of(k, q), q % 2)
            pos = base + q
            pick = r['pall'][pos]
            gate = r['grow'][pos]
            rows = dot(pick, r['dg'][s]).astype(BF16)
            for e in range(n_local):
                wide = pick[e * cap:(e + 1) * cap].astype(F32) * gate[e:e + 1, :]
                col = jnp.sum(wide, axis=1, keepdims=True)
                r['gcol'][e, pl.ds(pl.multiple_of(q * cap, 16), cap), :] = jnp.broadcast_to(col, (cap, 128))
                r['dyr'][e, pos_rows(pos, 1), :] = rows[e * cap:(e + 1) * cap]
            return carry

        lax.fori_loop(0, n, body, 0)

    def expert_fwd(k):
        base, n = spot(k)

        def body(e, carry):
            hidden = hidden_of(r['xr'][e, pos_rows(base, n), :], r['w1'][e], r['w3'][e])[2]
            r['rowbuf'][e, 0:n * cap, :] = dot(hidden, r['w2'][e]).astype(BF16)
            return carry

        lax.fori_loop(0, n_local, body, 0)

    def expert_bwd(k):
        base, n = spot(k)

        def body(e, carry):
            span = pos_rows(base, n)
            here = slice(0, n * cap)
            pre_gate, pre_up, hidden = hidden_of(r['xr'][e, span, :], r['w1'][e], r['w3'][e])
            dy = r['dyr'][e, span, :]
            projected = dot_nt(dy, r['w2'][e])
            gcol = r['gcol'][e, here, 0:1]
            dgate = jnp.sum(hidden.astype(F32) * projected, axis=1, keepdims=True)
            r['gcol'][e, here, :] = jnp.broadcast_to(dgate, (n * cap, 128))
            r['dyr'][e, span, :] = (gcol * dy.astype(F32)).astype(BF16)
            da_gate, da_up = swiglu_grads(pre_gate, pre_up, gcol * projected)
            r['h'][e, span, :] = hidden
            r['da1'][e, span, :] = da_gate
            r['da3'][e, span, :] = da_up
            du = dot(da_gate, r['w1'][e]) + dot(da_up, r['w3'][e])
            r['rowbuf'][e, here, :] = du.astype(BF16)
            return carry

        lax.fori_loop(0, n_local, body, 0)

    def combine(k, sc, gated, frees):
        base, n = spot(k)
        sc.free(frees)
        for ridx in range(n // 2):
            offset = offset_of(k, 2 * ridx)
            roff = offset % nz if isinstance(offset, int) else lax.rem(offset + nz, nz)
            for rel in (1, 0):
                q = 2 * ridx + rel
                pos = base + q
                rows = jnp.concatenate([r['rowbuf'][e, q * cap:(q + 1) * cap, :] for e in range(n_local)], axis=0)
                if gated:
                    pick = r['pall'][pos].astype(F32)
                    gate = r['grow'][pos]
                    part = None
                    for _ in range(3):
                        term = gate.astype(BF16).astype(F32)
                        gate = gate - term
                        wide = jnp.concatenate(
                            [pick[e * cap:(e + 1) * cap] * term[e:e + 1, :] for e in range(n_local)], axis=0)
                        one = dot_tn(wide.astype(BF16), rows)
                        part = one if part is None else part + one
                else:
                    part = dot_tn(r['pall'][pos], rows)
                if rel == 1:
                    sc.out[ridx] = part
                else:
                    sc.acc[roff] = part
            sc.cross(roff, ridx).start()

    def gate_rows(k, dgout):
        base, n = spot(k)

        def body(q, carry):
            s = p.source(offset_of(k, q), q % 2)
            pos = base + q
            rows = []
            for e in range(n_local):
                col = r['gcol'][e, pl.ds(pl.multiple_of(q * cap, 16), cap), 0:1]
                pick = r['pall'][pos, e * cap:(e + 1) * cap, :].astype(F32)
                rows.append(jnp.sum(pick * col, axis=0, keepdims=True))
            wide = jnp.concatenate(rows, axis=0)
            half = tokens // 2
            dgout[s] = jnp.concatenate([wide[:, :half], wide[:, half:]], axis=0)
            return carry

        lax.fori_loop(0, n, body, 0)

    def upward(k, first):
        return [(0, k - 1, k > first), (1, lax.rem(nz - (k - 1), nz), k > max(first, 1))]

    def order(j):
        return 3 + 2 * (j // 2) - j % 2

    def turn(sc, j):
        i = order(j)
        when(j % 2 == 0, lambda: sc.merge_for(i))
        sc.step(i)

    turns = nz - 4

    def phase(fwd, bwd, layer, tag, early, emit_y, emit_dx):
        weights = load_weights(tag)
        for copy in weights:
            copy.start()
        streams = [xs, ds] if bwd else [tabs, xs]
        x_streams = [xs] if bwd else [tabs, xs]
        dgout, dgin, a_ss, a_rs = (r[n] for n in ('dgout', 'dgin' + tag, 'as' + tag, 'ar' + tag)) if bwd else (None,) * 4

        for copy in weights[:3]:
            copy.wait()
        x_own = r['xg'][p.me]
        s_gate, s_up, s_hidden = hidden_of(x_own, r['ws1'][...], r['ws3'][...])
        if fwd:
            r['sh'][...] = dot(s_hidden, r['ws2'][...]) + x_own.astype(F32)
        if bwd:
            d_own = r['dg'][p.me]
            d_sg, d_su = swiglu_grads(s_gate, s_up, dot_nt(d_own, r['ws2'][...]))
            r['shd'][...] = dot(d_sg, r['ws1'][...]) + dot(d_su, r['ws3'][...]) + d_own.astype(F32)
            route(0, layer)
            lax.fori_loop(1, far, lambda k, c: (route(k, layer), c)[1], 0)
            route(far, layer)
        for copy in weights[3:]:
            copy.wait()

        def group_x(k, frees):
            for st in x_streams:
                arrived(st, k)
            if not bwd:
                route(k, layer)
            dispatch(k)
            if fwd:
                expert_fwd(k)
                combine(k, sf, True, frees)

        def group_dy(k, frees):
            arrived(ds, k)
            dispatch_dy(k)
            expert_bwd(k)
            combine(k, sb, False, frees)
            gate_rows(k, dgout)

        def steps(k):
            for st in streams:
                st.step(k)

        first = 0 if bwd else 1
        if bwd:
            group_x(0, [])
            if not fwd:
                group_dy(0, [])

        def middle(k, carry):
            steps(k)
            group_x(k, upward(k, first))
            if not fwd:
                group_dy(k, upward(k, first))
            return carry

        lax.fori_loop(1, far, middle, 0)
        steps(far)
        lead = sf if fwd else sb
        lead.begin(1)
        last = [(0, far - 1, True)]
        group_x(far, last)
        if not fwd:
            group_dy(far, last)
        lead.begin(0)
        left = [(lead, 0, far), (lead, 1, nz - far + 1)]

        def grad_copy(o, wait):
            to = lax.rem(p.me + o, n_dev)
            landed = dgin.at[lax.rem(p.me - o + n_dev, n_dev)] if wait else dgin.at[p.me]
            return pltpu.make_async_remote_copy(dgout.at[to], landed, a_ss.at[o], a_rs.at[o],
                                                device_id={'ep': to}, device_id_type=MESH)

        def put(e):
            return [pltpu.make_async_copy(r['g' + n], r[n + tag].at[e], r['osem'].at[i])
                    for i, n in enumerate(('dw1', 'dw3', 'dw2'))]

        def weight_grads(e):
            copies = put(e)

            @pl.when(e > 0)
            def _():
                for copy in copies:
                    copy.wait()

            rows = r['xr'][e]
            r['gdw1'][...] = dot_tn(r['da1'][e], rows)
            r['gdw3'][...] = dot_tn(r['da3'][e], rows)
            r['gdw2'][...] = dot_tn(r['h'][e], r['dyr'][e])
            for copy in copies:
                copy.start()

        def drain_streams():
            for st in streams:
                st.drain()

        if not bwd:
            turn(sf, 0)
            drain_streams()
            group_x(0, [(0, far, True)])
            left[0] = (sf, 0, 0)
            for j in range(1, turns):
                turn(sf, j)
            sf.step(nz - 2)
        else:
            if fwd:
                group_dy(far, [])
                turn(sf, 0)
                group_dy(far - 1, [(0, far, True)])
                turn(sf, 1)
                sb.begin(1)
                sb.begin(0)

                def outward(j, carry):
                    k = far - j
                    group_dy(k, [(0, k + 1, True), (1, nz - (k + 1), True)])
                    turn(sf, j)
                    return carry

                lax.fori_loop(2, far, outward, 0)
                drain_streams()
                group_dy(0, [(0, 1, True)])
                left += [(sb, 0, 0), (sb, 1, nz - 1)]
                sf.step(nz - 2)

            def push(o, carry):
                grad_copy(o, False).start()
                return carry

            lax.fori_loop(1, n_dev, push, 0)

            def ring(j, carry):
                turn(sb, j)
                weight_grads(j)
                return carry

            lax.fori_loop(0, turns, ring, 0)
            sb.step(nz - 2)
        if not fwd:
            drain_streams()
        if fwd:
            sf.merge(0)
        if bwd:
            sb.merge(0)
        early()
        if bwd:
            dgin[p.me] = dgout[p.me]

            def pull(o, carry):
                grad_copy(o, True).wait_recv()
                return carry

            lax.fori_loop(1, n_dev, pull, 0)
            ids = r['tab'][p.me, pl.ds(layer * TAB, TAB), :]

            def collect(dev, total):
                block = dgin[dev]
                wide = jnp.concatenate([block[:n_local], block[n_local:]], axis=1)
                for e in range(n_local):
                    total += jnp.where(ids == (dev * n_local + e).astype(F32), wide[e:e + 1, :], 0.0)
                return total

            r['dgate' + tag][...] = lax.fori_loop(0, n_dev, collect, jnp.zeros((TAB, tokens), F32))
        if fwd:
            sf.finish()
            emit_y(r['sh'][...] + sf.acc[0])
        if bwd:
            sb.finish()
            emit_dx(r['shd'][...] + sb.acc[0])
            for copy in put(n_local - 1):
                copy.wait()

            def done(o, carry):
                grad_copy(o, False).wait_send()
                return carry

            lax.fori_loop(1, n_dev, done, 0)
        for sc, slot, roff in left:
            sc.cross(roff, slot).wait_send()
        if fwd:
            sf.drain()
        if bwd:
            sb.drain()

    def store(name, index=None):
        def put(value):
            if index is None:
                r[name][...] = value.astype(BF16)
            else:
                r[name][index] = value.astype(BF16)
        return put

    def early_a():
        own_dy.wait()
        ds.start()

    phase(True, False, 0, '_a', early_a, store('xg', p.me), None)
    xs.start()

    again = load_own('x_in', 'xg', 1)

    def early_b():
        again.start()
        again.wait()
        xs.start()

    phase(True, True, 1, '_b', early_b, store('y_out'), store('dg', p.me))
    ds.start()

    phase(False, True, 0, '_a', lambda: None, None, store('dx_out'))


def run_step(dims, x, dy, tab, weights_a, weights_b):
    nz, n_local, cap, tokens = dims
    n_dev = 2 * nz
    d = x.shape[1]
    f = weights_a[0].shape[1]
    slots = n_local * cap
    rows = n_dev * cap
    any_spec = pl.BlockSpec(memory_space=pl.ANY)
    vmem_spec = pl.BlockSpec(memory_space=pltpu.VMEM)
    dma = pltpu.SemaphoreType.DMA
    kinds = ('w1', 'w3', 'w2', 'ws1', 'ws3', 'ws2')
    ins = {'x_in': x, 'dy_in': dy, 'tab_in': tab}
    ins.update({n + '_a': w for n, w in zip(kinds, weights_a)})
    ins.update({n + '_b': w for n, w in zip(kinds, weights_b)})
    outs = {'y_out': ((tokens, d), BF16, vmem_spec), 'dx_out': ((tokens, d), BF16, vmem_spec)}
    for tag in ('_a', '_b'):
        for n in ('dw1', 'dw3', 'dw2'):
            outs[n + tag] = ((n_local, f, d), F32, any_spec)
        outs['dgate' + tag] = ((TAB, tokens), F32, vmem_spec)
    scratch = {n: pltpu.VMEM(w.shape, BF16) for n, w in zip(kinds, weights_a)}
    scratch.update({
        'lsem': dma((3,)), 'wsem': dma((6,)), 'osem': dma((3,)),
        'xg': pltpu.VMEM((n_dev, tokens, d), BF16),
        'dg': pltpu.VMEM((n_dev, tokens, d), BF16),
        'tab': pltpu.VMEM((n_dev, 4 * TAB, tokens), F32),
        'tri': pltpu.VMEM((tokens, tokens), BF16),
        'pall': pltpu.VMEM((n_dev, slots, tokens), BF16),
        'grow': pltpu.VMEM((n_dev, 8, tokens), F32),
        'xr': pltpu.VMEM((n_local, rows, d), BF16),
        'dyr': pltpu.VMEM((n_local, rows, d), BF16),
        'rowbuf': pltpu.VMEM((n_local, 4 * cap, d), BF16),
        'gcol': pltpu.VMEM((n_local, 4 * cap, 128), F32),
        'h': pltpu.VMEM((n_local, rows, f), BF16),
        'da1': pltpu.VMEM((n_local, rows, f), BF16),
        'da3': pltpu.VMEM((n_local, rows, f), BF16),
        'gdw1': pltpu.VMEM((f, d), F32), 'gdw3': pltpu.VMEM((f, d), F32), 'gdw2': pltpu.VMEM((f, d), F32),
        'dgout': pltpu.VMEM((n_dev, 2 * n_local, tokens // 2), F32),
        'sh': pltpu.VMEM((tokens, d), F32), 'shd': pltpu.VMEM((tokens, d), F32),
        'gs': dma((2, 2, nz // 2)), 'gr': dma((2, 2, nz // 2)), 'gxs': dma((nz, 2)), 'gxr': dma((nz, 2)),
        'ds': dma((2, 2, nz // 2)), 'dr': dma((2, 2, nz // 2)), 'dxs': dma((nz, 2)), 'dxr': dma((nz, 2)),
        'ts': dma((2, 1, nz // 2)), 'tr': dma((2, 1, nz // 2)), 'txs': dma((nz, 1)), 'txr': dma((nz, 1)),
    })
    for tag in ('_a', '_b'):
        scratch.update({
            'dgin' + tag: pltpu.VMEM((n_dev, 2 * n_local, tokens // 2), F32),
            'as' + tag: dma((n_dev,)), 'ar' + tag: dma((n_dev,)),
        })
    for tag in ('f', 'b'):
        scratch.update({
            tag + 'acc': pltpu.VMEM((nz, tokens, d), F32),
            tag + 'out': pltpu.VMEM((2, tokens, d), F32),
            tag + 'sib': pltpu.VMEM((nz, tokens, d), F32),
            tag + 'box': pltpu.VMEM((2, nz - 1, tokens // 2, d), F32),
            tag + 'xs': dma((nz,)), tag + 'xr': dma((nz,)),
            tag + 'ss': dma((2, nz - 1)), tag + 'rs': dma((2, nz - 1)),
        })
    result = pl.pallas_call(
        functools.partial(step_kernel, list(ins) + list(outs) + list(scratch), dims),
        out_shape=[jax.ShapeDtypeStruct(s, t) for s, t, _ in outs.values()],
        in_specs=[any_spec] * len(ins),
        out_specs=[spec for _, _, spec in outs.values()],
        scratch_shapes=list(scratch.values()),
        compiler_params=pltpu.CompilerParams(collective_id=0, has_side_effects=True, vmem_limit_bytes=VMEM_BYTES),
        name='two_layers',
    )(*ins.values())
    return dict(zip(outs, result))


def settle_kernel(pieces, *refs):
    n = len(refs[:-2]) // 3
    ins, outs, bufs = refs[:n], refs[n:2 * n], refs[2 * n:3 * n]
    get_sem, put_sem = refs[-2:]
    gets, puts = [], []
    for i in range(n):
        for j in range(pieces[i]):
            rows = pl.ds(j * (ins[i].shape[0] // pieces[i]), ins[i].shape[0] // pieces[i])
            at = len(gets)
            gets.append(pltpu.make_async_copy(ins[i].at[rows], bufs[i].at[rows], get_sem.at[at]))
            puts.append(pltpu.make_async_copy(bufs[i].at[rows], outs[i].at[rows], put_sem.at[at]))
    for get in gets:
        get.start()
    for get, put in zip(gets, puts):
        get.wait()
        put.start()
    for put in puts:
        put.wait()


def settle(arrays):
    pieces = [a.shape[0] if a.ndim == 3 else 1 for a in arrays]
    total = sum(pieces)
    any_spec = pl.BlockSpec(memory_space=pl.ANY)
    return pl.pallas_call(
        functools.partial(settle_kernel, pieces),
        out_shape=[jax.ShapeDtypeStruct(a.shape, a.dtype) for a in arrays],
        in_specs=[any_spec] * len(arrays),
        out_specs=[any_spec] * len(arrays),
        scratch_shapes=[pltpu.VMEM(a.shape, a.dtype) for a in arrays]
        + [pltpu.SemaphoreType.DMA((total,)), pltpu.SemaphoreType.DMA((total,))],
        compiler_params=pltpu.CompilerParams(vmem_limit_bytes=VMEM_BYTES),
        name='settle',
    )(*arrays)


def solution(mesh):
    group_size = mesh.shape['ep']
    token_spec = P(('dp', 'ep'), None)
    expert_spec = P('ep', None, None)
    shared_spec = P(None, None)
    grad_spec = P(('dp', 'ep'), None, None)
    layer_specs = (expert_spec,) * 3 + (shared_spec,) * 3

    def device_step(x_in, d_out, idx_a, gate_a, idx_b, gate_b,
                    w1_a, w3_a, w2_a, ws1_a, ws3_a, ws2_a,
                    w1_b, w3_b, w2_b, ws1_b, ws3_b, ws2_b):
        def turned(w):
            return jnp.swapaxes(w, -1, -2)

        weights_a = (turned(w1_a), turned(w3_a), w2_a, turned(ws1_a), turned(ws3_a), ws2_a)
        weights_b = (turned(w1_b), turned(w3_b), w2_b, turned(ws1_b), turned(ws3_b), ws2_b)
        tokens, top_k = idx_a.shape
        n_local = w1_a.shape[0]
        dims = (group_size // 2, n_local, slot_capacity(tokens, n_local * group_size, top_k), tokens)

        def padded(values, fill):
            return jnp.pad(values.astype(F32), ((0, 0), (0, TAB - top_k)), constant_values=fill)

        table = jnp.concatenate([padded(idx_a, -1.0), padded(idx_b, -1.0), padded(gate_a, 0.0), padded(gate_b, 0.0)],
                                axis=1).T
        got = run_step(dims, x_in, d_out, table, weights_a, weights_b)
        x_last, d_first, *grads = settle(
            [got['y_out'], got['dx_out']] + [got[n + tag] for tag in ('_a', '_b') for n in ('dw1', 'dw3', 'dw2')])
        for at in (0, 1, 3, 4):
            grads[at] = turned(grads[at])
        return (x_last, d_first, *grads, got['dgate_a'][:top_k].T, got['dgate_b'][:top_k].T)

    in_specs = (token_spec,) * 6 + layer_specs + layer_specs
    out_specs = (token_spec, token_spec) + (grad_spec,) * 6 + (token_spec, token_spec)
    return jax.shard_map(device_step, mesh=mesh, in_specs=in_specs, out_specs=out_specs, check_vma=False)
```

time: 336 us -> 323 us (0.961)
  Pallas kernels: 332 us -> 318 us
    pallas_call x3 -> x1, Pallas kernels: 319 us -> 305 us  [run_step(): pl.pallas_call(functools.partial(step_kernel, list(ins) + list(outs) + li...]
where the time goes in v4:
time: 323 us; the launch traced here: 322 us
  Pallas kernels  318 us (98%)
    pallas_call x1, Pallas kernels, run_step(): pl.pallas_call(functools.partial(step_kernel, list(ins) + list(outs) + li...  305 us
    pallas_call x1, Pallas kernels, settle(): pl.pallas_call(functools.partial(settle_kernel, pieces), out_shape=[jax.S...  13 us

profile of v4, /device:TPU:21, one launch (start us, length us, event | category | flops | bytes accessed | tf_op | source)
XLA Modules:
  0.0 322.4 jit_solution(15278314423615573508)
XLA Ops:
  0.6 0.7 convert_element_type.6
  1.3 0.7 convert_element_type.7
  2.0 1.3 fusion.refs_2_
  3.4 305.4 %two_layers.1 = (bf16[256,512]{1,0:T(8,128)(2,1)}, bf16[256,512]{1,0:T(8,128)(2,1)}, f32[4,352,512]{2,1,0:T(8,128)}, f32[4,352,512]{2,1,0:T(8,128)}, f32[4,352,5...) custom-call(bf16[256,512]{1,0:T(8,128)(2,1)} %refs_0_.1, ...), custom_call_target="tpu_custom_call" | custom-call | tf_op jit(solution)/shard_map/two_layers/pallas_call | solution.py:688
  308.8 0.0 copy-start
  308.8 0.0 copy-start.1
  308.8 13.0 %settle.1 = (bf16[256,512]{1,0:T(8,128)(2,1)}, bf16[256,512]{1,0:T(8,128)(2,1)}, f32[4,352,512]{2,1,0:T(8,128)}, f32[4,352,512]{2,1,0:T(8,128)}, f32[4,352,512]{...) custom-call(bf16[256,512]{1,0:T(8,128)(2,1)} %get-tuple-element.28.refs_0_, ...), custom_call_target="tpu_custom_call" | custom-call | tf_op jit(solution)/shard_map/settle/pallas_call | solution.py:724
  321.8 0.0 copy-done
  321.8 0.0 copy-done.1
  321.8 0.6 slice_bitcast_fusion
Async XLA Ops:
  308.8 13.0 %copy-start = (f32[8,256]{1,0:T(8,128)S(1)}, f32[8,256]{1,0:T(8,128)}, u32[]{:S(2)}) copy-start(f32[8,256]{1,0:T(8,128)} %get-tuple-element.44) | copy-start | bytes 24580
  308.8 13.0 %copy-start.1 = (f32[8,256]{1,0:T(8,128)S(1)}, f32[8,256]{1,0:T(8,128)}, u32[]{:S(2)}) copy-start(f32[8,256]{1,0:T(8,128)} %get-tuple-element.45) | copy-start | bytes 24580

commit v5 on v4

--- a/solution.py
+++ b/solution.py
@@ -12,6 +12,7 @@
 MESH = pl.DeviceIdType.MESH
 VMEM_BYTES = 67_000_000
 TAB = 8
+PARTS = 2
 
 
 def slot_capacity(tokens, n_experts, top_k):
@@ -165,33 +166,32 @@
     def side(self, di, i):
         return (i + di) % 2
 
-    def hop(self, di, i):
-        rows = pl.ds(self.side(di, i) * self.half, self.half)
-        return pltpu.make_async_remote_copy(self.acc.at[self.roff(di, i), rows], self.box.at[di, i],
-                                            self.ss.at[di, i], self.rs.at[di, i],
+    def hop(self, di, i, part):
+        size = self.half // PARTS
+        rows = pl.ds(self.side(di, i) * self.half + part * size, size)
+        return pltpu.make_async_remote_copy(self.acc.at[self.roff(di, i), rows],
+                                            self.box.at[di, i, pl.ds(part * size, size)],
+                                            self.ss.at[di, i, part], self.rs.at[di, i, part],
                                             device_id=self.p.device(1 - 2 * di), device_id_type=MESH)
 
-    def take(self, di, i, roff):
-        self.hop(di, i).wait_recv()
-        first = self.side(di, i) * self.half
-
-        def add(j, carry):
-            rows = pl.ds(pl.multiple_of(first + j * 64, 64), 64)
-            self.acc[roff, rows, :] += self.box[di, i, pl.ds(j * 64, 64), :]
-            return carry
-
-        lax.fori_loop(0, self.half // 64, add, 0)
+    def take(self, di, i, part, roff):
+        self.hop(di, i, part).wait_recv()
+        size = self.half // PARTS
+        into = pl.ds(pl.multiple_of(self.side(di, i) * self.half + part * size, size), size)
+        self.acc[roff, into, :] += self.box[di, i, pl.ds(part * size, size), :]
 
     def begin(self, i):
         for roff in sorted({self.roff(0, i), self.roff(1, i)}):
             self.merge(roff)
-        for di in range(2):
-            self.hop(di, i).start()
+        for part in range(PARTS):
+            for di in range(2):
+                self.hop(di, i, part).start()
 
     def step(self, i):
-        for di in range(2):
-            self.take(di, i - 2, self.roff(di, i))
-            self.hop(di, i).start()
+        for part in range(PARTS):
+            for di in range(2):
+                self.take(di, i - 2, part, self.roff(di, i))
+                self.hop(di, i, part).start()
 
     def merge_for(self, i):
         self.merge(self.roff(0, i))
@@ -203,18 +203,20 @@
 
     def finish(self):
         for i in (self.steps - 2, self.steps - 1):
-            for di in range(2):
-                self.take(di, i, 0)
+            for part in range(PARTS):
+                for di in range(2):
+                    self.take(di, i, part, 0)
 
     def drain(self):
         for i in range(self.steps):
-            for di in range(2):
-                self.hop(di, i).wait_send()
+            for part in range(PARTS):
+                for di in range(2):
+                    self.hop(di, i, part).wait_send()
 
 
 def step_kernel(names, dims, *refs):
     r = dict(zip(names, refs))
-    nz, n_local, cap, tokens = dims
+    nz, n_local, cap, tokens, top_k = dims
     p = Place(nz)
     n_dev = 2 * nz
     far = nz // 2
@@ -226,15 +228,21 @@
     def load_own(name, buf, i):
         return pltpu.make_async_copy(r[name], r[buf].at[p.me], r['lsem'].at[i])
 
-    own = [load_own('tab_in', 'tab', 0), load_own('x_in', 'xg', 1)]
-    own_dy = load_own('dy_in', 'dg', 2)
-    for copy in own + [own_dy]:
+    own_x, own_dy = load_own('x_in', 'xg', 1), load_own('dy_in', 'dg', 2)
+    parts = [pltpu.make_async_copy(r[n + '_in'], r[n], r['tsem'].at[i])
+             for i, n in enumerate(('idx_a', 'idx_b', 'gate_a', 'gate_b'))]
+    for copy in parts + [own_x, own_dy]:
         copy.start()
+    for i, (copy, name) in enumerate(zip(parts, ('idx_a', 'idx_b', 'gate_a', 'gate_b'))):
+        copy.wait()
+        rows = r[name][...].astype(F32)
+        fill = jnp.full((TAB - rows.shape[0], tokens), -1.0 if i < 2 else 0.0, F32)
+        r['tab'][p.me, i * TAB:(i + 1) * TAB, :] = jnp.concatenate([rows, fill], axis=0)
 
     barrier = pltpu.get_barrier_semaphore()
-    for o in range(1, n_dev):
-        pl.semaphore_signal(barrier, inc=1, device_id={'ep': lax.rem(p.me + o, n_dev)}, device_id_type=MESH)
-    pl.semaphore_wait(barrier, n_dev - 1)
+    for peer in (p.device(1), p.device(-1), p.device(0, 1)):
+        pl.semaphore_signal(barrier, inc=1, device_id=peer, device_id_type=MESH)
+    pl.semaphore_wait(barrier, 3)
 
     tabs = Gather(p, r['tab'], 1, (r['ts'], r['tr'], r['txs'], r['txr']))
     xs = Gather(p, r['xg'], 2, (r['gs'], r['gr'], r['gxs'], r['gxr']))
@@ -242,8 +250,7 @@
     sf = Scatter(p, r['facc'], r['fout'], r['fsib'], r['fbox'], (r['fxs'], r['fxr'], r['fss'], r['frs']))
     sb = Scatter(p, r['bacc'], r['bout'], r['bsib'], r['bbox'], (r['bxs'], r['bxr'], r['bss'], r['brs']))
 
-    for copy in own:
-        copy.wait()
+    own_x.wait()
     tabs.start()
     xs.start()
 
@@ -415,7 +422,7 @@
 
     turns = nz - 4
 
-    def phase(fwd, bwd, layer, tag, early, emit_y, emit_dx):
+    def phase(fwd, bwd, layer, tag, middle_hook, early, emit_y, emit_dx):
         weights = load_weights(tag)
         for copy in weights:
             copy.start()
@@ -457,8 +464,15 @@
             gate_rows(k, dgout)
 
         def steps(k):
-            for st in streams:
+            for st in x_streams:
                 st.step(k)
+            if bwd and not fwd:
+                ds.step(k)
+            elif bwd:
+                if isinstance(k, int):
+                    ds.step(k)
+                else:
+                    when(k + 1 < far, lambda: ds.step(k + 1))
 
         first = 0 if bwd else 1
         if bwd:
@@ -475,6 +489,7 @@
 
         lax.fori_loop(1, far, middle, 0)
         steps(far)
+        middle_hook()
         lead = sf if fwd else sb
         lead.begin(1)
         last = [(0, far - 1, True)]
@@ -579,7 +594,7 @@
                     total += jnp.where(ids == (dev * n_local + e).astype(F32), wide[e:e + 1, :], 0.0)
                 return total
 
-            r['dgate' + tag][...] = lax.fori_loop(0, n_dev, collect, jnp.zeros((TAB, tokens), F32))
+            r['dgate' + tag][...] = lax.fori_loop(0, n_dev, collect, jnp.zeros((TAB, tokens), F32))[:top_k]
         if fwd:
             sf.finish()
             emit_y(r['sh'][...] + sf.acc[0])
@@ -609,28 +624,31 @@
                 r[name][index] = value.astype(BF16)
         return put
 
-    def early_a():
+    def nothing():
+        pass
+
+    def send_dy():
         own_dy.wait()
         ds.start()
 
-    phase(True, False, 0, '_a', early_a, store('xg', p.me), None)
+    phase(True, False, 0, '_a', send_dy, lambda: ds.step(1), store('xg', p.me), None)
     xs.start()
 
     again = load_own('x_in', 'xg', 1)
 
-    def early_b():
+    def send_x():
         again.start()
         again.wait()
         xs.start()
 
-    phase(True, True, 1, '_b', early_b, store('y_out'), store('dg', p.me))
+    phase(True, True, 1, '_b', nothing, send_x, store('y_out'), store('dg', p.me))
     ds.start()
 
-    phase(False, True, 0, '_a', lambda: None, None, store('dx_out'))
-
-
-def run_step(dims, x, dy, tab, weights_a, weights_b):
-    nz, n_local, cap, tokens = dims
+    phase(False, True, 0, '_a', nothing, nothing, None, store('dx_out'))
+
+
+def run_step(dims, x, dy, routes, weights_a, weights_b):
+    nz, n_local, cap, tokens, top_k = dims
     n_dev = 2 * nz
     d = x.shape[1]
     f = weights_a[0].shape[1]
@@ -640,17 +658,19 @@
     vmem_spec = pl.BlockSpec(memory_space=pltpu.VMEM)
     dma = pltpu.SemaphoreType.DMA
     kinds = ('w1', 'w3', 'w2', 'ws1', 'ws3', 'ws2')
-    ins = {'x_in': x, 'dy_in': dy, 'tab_in': tab}
+    ins = {'x_in': x, 'dy_in': dy}
+    ins.update({n + '_in': a for n, a in routes.items()})
     ins.update({n + '_a': w for n, w in zip(kinds, weights_a)})
     ins.update({n + '_b': w for n, w in zip(kinds, weights_b)})
     outs = {'y_out': ((tokens, d), BF16, vmem_spec), 'dx_out': ((tokens, d), BF16, vmem_spec)}
     for tag in ('_a', '_b'):
         for n in ('dw1', 'dw3', 'dw2'):
             outs[n + tag] = ((n_local, f, d), F32, any_spec)
-        outs['dgate' + tag] = ((TAB, tokens), F32, vmem_spec)
+        outs['dgate' + tag] = ((top_k, tokens), F32, vmem_spec)
     scratch = {n: pltpu.VMEM(w.shape, BF16) for n, w in zip(kinds, weights_a)}
     scratch.update({
-        'lsem': dma((3,)), 'wsem': dma((6,)), 'osem': dma((3,)),
+        **{n: pltpu.VMEM(a.shape, a.dtype) for n, a in routes.items()},
+        'tsem': dma((4,)), 'lsem': dma((3,)), 'wsem': dma((6,)), 'osem': dma((3,)),
         'xg': pltpu.VMEM((n_dev, tokens, d), BF16),
         'dg': pltpu.VMEM((n_dev, tokens, d), BF16),
         'tab': pltpu.VMEM((n_dev, 4 * TAB, tokens), F32),
@@ -683,7 +703,7 @@
             tag + 'sib': pltpu.VMEM((nz, tokens, d), F32),
             tag + 'box': pltpu.VMEM((2, nz - 1, tokens // 2, d), F32),
             tag + 'xs': dma((nz,)), tag + 'xr': dma((nz,)),
-            tag + 'ss': dma((2, nz - 1)), tag + 'rs': dma((2, nz - 1)),
+            tag + 'ss': dma((2, nz - 1, PARTS)), tag + 'rs': dma((2, nz - 1, PARTS)),
         })
     result = pl.pallas_call(
         functools.partial(step_kernel, list(ins) + list(outs) + list(scratch), dims),
@@ -751,19 +771,16 @@
         weights_b = (turned(w1_b), turned(w3_b), w2_b, turned(ws1_b), turned(ws3_b), ws2_b)
         tokens, top_k = idx_a.shape
         n_local = w1_a.shape[0]
-        dims = (group_size // 2, n_local, slot_capacity(tokens, n_local * group_size, top_k), tokens)
-
-        def padded(values, fill):
-            return jnp.pad(values.astype(F32), ((0, 0), (0, TAB - top_k)), constant_values=fill)
-
-        table = jnp.concatenate([padded(idx_a, -1.0), padded(idx_b, -1.0), padded(gate_a, 0.0), padded(gate_b, 0.0)],
-                                axis=1).T
-        got = run_step(dims, x_in, d_out, table, weights_a, weights_b)
+        dims = (group_size // 2, n_local, slot_capacity(tokens, n_local * group_size, top_k), tokens, top_k)
+        routes = {'idx_a': idx_a.T, 'idx_b': idx_b.T, 'gate_a': gate_a.T, 'gate_b': gate_b.T}
+        got = run_step(dims, x_in, d_out, routes, weights_a, weights_b)
         x_last, d_first, *grads = settle(
-            [got['y_out'], got['dx_out']] + [got[n + tag] for tag in ('_a', '_b') for n in ('dw1', 'dw3', 'dw2')])
+            [got['y_out'], got['dx_out']]
+            + [got[n + tag] for tag in ('_a', '_b') for n in ('dw1', 'dw3', 'dw2')]
+            + [got['dgate_a'], got['dgate_b']])
         for at in (0, 1, 3, 4):
             grads[at] = turned(grads[at])
-        return (x_last, d_first, *grads, got['dgate_a'][:top_k].T, got['dgate_b'][:top_k].T)
+        return (x_last, d_first, *grads[:6], grads[6].T, grads[7].T)
 
     in_specs = (token_spec,) * 6 + layer_specs + layer_specs
     out_specs = (token_spec, token_spec) + (grad_spec,) * 6 + (token_spec, token_spec)

time: 323 us -> 315 us (0.975)
  Pallas kernels: 318 us -> 314 us
    pallas_call x1, Pallas kernels: 305 us -> 301 us  [run_step(): pl.pallas_call(functools.partial(step_kernel, list(ins) + list(outs) + li...]
where the time goes in v5:
time: 315 us
  Pallas kernels  314 us (100%)
    pallas_call x1, Pallas kernels, run_step(): pl.pallas_call(functools.partial(step_kernel, list(ins) + list(outs) + li...  301 us
    pallas_call x1, Pallas kernels, settle(): pl.pallas_call(functools.partial(settle_kernel, pieces), out_shape=[jax.S...  13 us

profile of v5, /device:TPU:21, one launch (start us, length us, event | category | flops | bytes accessed | tf_op | source)
XLA Modules:
  0.0 314.7 jit_solution(9895901887190774976)
XLA Ops:
  0.7 300.8 %two_layers.1 = (bf16[256,512]{1,0:T(8,128)(2,1)}, bf16[256,512]{1,0:T(8,128)(2,1)}, f32[4,352,512]{2,1,0:T(8,128)}, f32[4,352,512]{2,1,0:T(8,128)}, f32[4,352,5...) custom-call(bf16[256,512]{1,0:T(8,128)(2,1)} %refs_0_.1, ...), custom_call_target="tpu_custom_call" | custom-call | tf_op jit(solution)/shard_map/two_layers/pallas_call | solution.py:708
  301.5 13.0 %settle.1 = (bf16[256,512]{1,0:T(8,128)(2,1)}, bf16[256,512]{1,0:T(8,128)(2,1)}, f32[4,352,512]{2,1,0:T(8,128)}, f32[4,352,512]{2,1,0:T(8,128)}, f32[4,352,512]{...) custom-call(bf16[256,512]{1,0:T(8,128)(2,1)} %get-tuple-element.30.r, ...), custom_call_target="tpu_custom_call" | custom-call | tf_op jit(solution)/shard_map/settle/pallas_call | solution.py:744

commit v6 on v5

--- a/solution.py
+++ b/solution.py
@@ -223,7 +223,7 @@
 
     def load_weights(tag):
         return [pltpu.make_async_copy(r[n + tag], r[n], r['wsem'].at[i])
-                for i, n in enumerate(('ws1', 'ws3', 'ws2', 'w1', 'w3', 'w2'))]
+                for i, n in enumerate(('w1', 'w3', 'w2', 'ws1', 'ws3', 'ws2'))]
 
     def load_own(name, buf, i):
         return pltpu.make_async_copy(r[name], r[buf].at[p.me], r['lsem'].at[i])
@@ -430,21 +430,24 @@
         x_streams = [xs] if bwd else [tabs, xs]
         dgout, dgin, a_ss, a_rs = (r[n] for n in ('dgout', 'dgin' + tag, 'as' + tag, 'ar' + tag)) if bwd else (None,) * 4
 
-        for copy in weights[:3]:
-            copy.wait()
-        x_own = r['xg'][p.me]
-        s_gate, s_up, s_hidden = hidden_of(x_own, r['ws1'][...], r['ws3'][...])
-        if fwd:
-            r['sh'][...] = dot(s_hidden, r['ws2'][...]) + x_own.astype(F32)
         if bwd:
-            d_own = r['dg'][p.me]
-            d_sg, d_su = swiglu_grads(s_gate, s_up, dot_nt(d_own, r['ws2'][...]))
-            r['shd'][...] = dot(d_sg, r['ws1'][...]) + dot(d_su, r['ws3'][...]) + d_own.astype(F32)
             route(0, layer)
             lax.fori_loop(1, far, lambda k, c: (route(k, layer), c)[1], 0)
             route(far, layer)
-        for copy in weights[3:]:
+        for copy in weights[:3]:
             copy.wait()
+
+        def shared():
+            for copy in weights[3:]:
+                copy.wait()
+            x_own = r['xg'][p.me]
+            s_gate, s_up, s_hidden = hidden_of(x_own, r['ws1'][...], r['ws3'][...])
+            if fwd:
+                r['sh'][...] = dot(s_hidden, r['ws2'][...]) + x_own.astype(F32)
+            if bwd:
+                d_own = r['dg'][p.me]
+                d_sg, d_su = swiglu_grads(s_gate, s_up, dot_nt(d_own, r['ws2'][...]))
+                r['shd'][...] = dot(d_sg, r['ws1'][...]) + dot(d_su, r['ws3'][...]) + d_own.astype(F32)
 
         def group_x(k, frees):
             for st in x_streams:
@@ -464,11 +467,17 @@
             gate_rows(k, dgout)
 
         def steps(k):
+            if bwd and not fwd:
+                ds.step(k)
+                if isinstance(k, int):
+                    xs.step(k)
+                else:
+                    when(k == 1, lambda: xs.step(2))
+                    when(k == far - 1, lambda: xs.step(far - 1))
+                return
             for st in x_streams:
                 st.step(k)
-            if bwd and not fwd:
-                ds.step(k)
-            elif bwd:
+            if bwd:
                 if isinstance(k, int):
                     ds.step(k)
                 else:
@@ -482,6 +491,8 @@
 
         def middle(k, carry):
             steps(k)
+            if middle_hook is not None:
+                pl.when(k == far - 1)(middle_hook)
             group_x(k, upward(k, first))
             if not fwd:
                 group_dy(k, upward(k, first))
@@ -489,7 +500,6 @@
 
         lax.fori_loop(1, far, middle, 0)
         steps(far)
-        middle_hook()
         lead = sf if fwd else sb
         lead.begin(1)
         last = [(0, far - 1, True)]
@@ -497,6 +507,7 @@
         if not fwd:
             group_dy(far, last)
         lead.begin(0)
+        shared()
         left = [(lead, 0, far), (lead, 1, nz - far + 1)]
 
         def grad_copy(o, wait):
@@ -641,10 +652,11 @@
         again.wait()
         xs.start()
 
-    phase(True, True, 1, '_b', nothing, send_x, store('y_out'), store('dg', p.me))
+    phase(True, True, 1, '_b', None, send_x, store('y_out'), store('dg', p.me))
     ds.start()
-
-    phase(False, True, 0, '_a', nothing, nothing, None, store('dx_out'))
+    xs.step(1)
+
+    phase(False, True, 0, '_a', None, nothing, None, store('dx_out'))
 
 
 def run_step(dims, x, dy, routes, weights_a, weights_b):

time: 315 us -> 308 us (0.978)
  Pallas kernels: 314 us -> 307 us
    pallas_call x1, Pallas kernels: 301 us -> 294 us  [run_step(): pl.pallas_call(functools.partial(step_kernel, list(ins) + list(outs) + li...]
where the time goes in v6:
time: 308 us
  Pallas kernels  307 us (100%)
    pallas_call x1, Pallas kernels, run_step(): pl.pallas_call(functools.partial(step_kernel, list(ins) + list(outs) + li...  294 us
    pallas_call x1, Pallas kernels, settle(): pl.pallas_call(functools.partial(settle_kernel, pieces), out_shape=[jax.S...  13 us

profile of v6, /device:TPU:21, one launch (start us, length us, event | category | flops | bytes accessed | tf_op | source)
XLA Modules:
  0.0 308.3 jit_solution(2879600681829442575)
XLA Ops:
  0.7 294.4 %two_layers.1 = (bf16[256,512]{1,0:T(8,128)(2,1)}, bf16[256,512]{1,0:T(8,128)(2,1)}, f32[4,352,512]{2,1,0:T(8,128)}, f32[4,352,512]{2,1,0:T(8,128)}, f32[4,352,5...) custom-call(bf16[256,512]{1,0:T(8,128)(2,1)} %refs_0_.1, ...), custom_call_target="tpu_custom_call" | custom-call | tf_op jit(solution)/shard_map/two_layers/pallas_call | solution.py:720
  295.1 13.0 %settle.1 = (bf16[256,512]{1,0:T(8,128)(2,1)}, bf16[256,512]{1,0:T(8,128)(2,1)}, f32[4,352,512]{2,1,0:T(8,128)}, f32[4,352,512]{2,1,0:T(8,128)}, f32[4,352,512]{...) custom-call(bf16[256,512]{1,0:T(8,128)(2,1)} %get-tuple-element.30.r, ...), custom_call_target="tpu_custom_call" | custom-call | tf_op jit(solution)/shard_map/settle/pallas_call | solution.py:756

commit v7 on v6

--- a/solution.py
+++ b/solution.py
@@ -627,12 +627,14 @@
         if bwd:
             sb.drain()
 
-    def store(name, index=None):
+    def store(name, index=None, then=None):
         def put(value):
             if index is None:
                 r[name][...] = value.astype(BF16)
             else:
                 r[name][index] = value.astype(BF16)
+            if then is not None:
+                then()
         return put
 
     def nothing():
@@ -642,8 +644,7 @@
         own_dy.wait()
         ds.start()
 
-    phase(True, False, 0, '_a', send_dy, lambda: ds.step(1), store('xg', p.me), None)
-    xs.start()
+    phase(True, False, 0, '_a', send_dy, lambda: ds.step(1), store('xg', p.me, xs.start), None)
 
     again = load_own('x_in', 'xg', 1)
 
@@ -652,8 +653,7 @@
         again.wait()
         xs.start()
 
-    phase(True, True, 1, '_b', None, send_x, store('y_out'), store('dg', p.me))
-    ds.start()
+    phase(True, True, 1, '_b', None, send_x, store('y_out'), store('dg', p.me, ds.start))
     xs.step(1)
 
     phase(False, True, 0, '_a', None, nothing, None, store('dx_out'))

time: 308 us -> 308 us (level)
  no operation moved by 1% of the time
where the time goes in v7:
time: 308 us
  Pallas kernels  307 us (100%)
    pallas_call x1, Pallas kernels, run_step(): pl.pallas_call(functools.partial(step_kernel, list(ins) + list(outs) + li...  294 us
    pallas_call x1, Pallas kernels, settle(): pl.pallas_call(functools.partial(settle_kernel, pieces), out_shape=[jax.S...  13 us

profile of v7, /device:TPU:21, one launch (start us, length us, event | category | flops | bytes accessed | tf_op | source)
XLA Modules:
  0.0 308.3 jit_solution(4161970573731524858)
XLA Ops:
  0.7 294.4 %two_layers.1 = (bf16[256,512]{1,0:T(8,128)(2,1)}, bf16[256,512]{1,0:T(8,128)(2,1)}, f32[4,352,512]{2,1,0:T(8,128)}, f32[4,352,512]{2,1,0:T(8,128)}, f32[4,352,5...) custom-call(bf16[256,512]{1,0:T(8,128)(2,1)} %refs_0_.1, ...), custom_call_target="tpu_custom_call" | custom-call | tf_op jit(solution)/shard_map/two_layers/pallas_call | solution.py:720
  295.1 13.0 %settle.1 = (bf16[256,512]{1,0:T(8,128)(2,1)}, bf16[256,512]{1,0:T(8,128)(2,1)}, f32[4,352,512]{2,1,0:T(8,128)}, f32[4,352,512]{2,1,0:T(8,128)}, f32[4,352,512]{...) custom-call(bf16[256,512]{1,0:T(8,128)(2,1)} %get-tuple-element.30.r, ...), custom_call_target="tpu_custom_call" | custom-call | tf_op jit(solution)/shard_map/settle/pallas_call | solution.py:756
